TPU v7x, 256 devices: a whole 4x4x8 slice. The times are simulated.
256 devices in a mesh: site: 2 (over y_lo), rows: 16 (over z, core), width: 8 (over y_hi, x).
Axes of the slice: x: 4, y: 4 (y_hi: 2, y_lo: 2; y = y_hi * 2 + y_lo), z: 8, core: 2. Of those that a mesh axis runs over, the one named last changes fastest.
Arguments:
- one_query: float32 [14336, 7168], P(('site', 'rows'), 'width'), parts along dimension 0, may hold values from -0.09375 to 0.09375
- other_query: float32 [14336, 7168], P(('site', 'rows'), 'width'), parts along dimension 0, may hold values from -0.0625 to 0.0625
- one_key: float32 [14336, 1024], P(('site', 'rows'), 'width'), parts along dimension 0, may hold values from -0.09375 to 0.09375
- other_key: float32 [14336, 1024], P(('site', 'rows'), 'width'), parts along dimension 0, may hold values from -0.0625 to 0.0625
- one_value: float32 [14336, 1024], P(('site', 'rows'), 'width'), parts along dimension 0, may hold values from -0.09375 to 0.09375
- other_value: float32 [14336, 1024], P(('site', 'rows'), 'width'), parts along dimension 0, may hold values from -0.0625 to 0.0625
- mix_share: float32 [14336], P(('site', 'rows')), parts along dimension 0, may hold values from 0.2 to 0.8
- norm_train: float32 [14336], P(('site', 'rows', 'width')), parts along dimension 0, may hold values from 0.25 to 1.75
- norm_step: float32 [14336], P(('site', 'rows', 'width')), parts along dimension 0, may hold values from -0.3 to 0.3
Outputs:
- serving_query: bfloat16 [14336, 7168], P('site', 'width'), parts along dimension 0
- serving_key: bfloat16 [14336, 1024], P('site', 'width'), parts along dimension 0
- serving_value: bfloat16 [14336, 1024], P('site', 'width'), parts along dimension 0
- scale_query: float32 [14336], P(('site', 'width')), parts along dimension 0
- scale_key: float32 [2048], P(('site', 'width')), parts along dimension 0
- scale_value: float32 [2048], P(('site', 'width')), parts along dimension 0
- serve_norm: bfloat16 [14336], P('site'), parts along dimension 0
There are 2 independent parts, one for each index of `site`. A program takes and returns all parts, laid end to end along the dimension named above; each array names one. Nothing has to cross between parts.
All inputs are finite; a program needn't handle non-finite values. Where the computation divides by a largest or mean magnitude, that divisor is 1e-20 or more.
Results may differ from a plain program's by a relative error of at most 0.001.
Values may be sent and summed in bfloat16 or wider, within the bound.
No kernel may reach another device: no remote copies, remote signals or barrier semaphores. Data moves between devices by JAX's collectives and lax.ppermute only.
A program may use at most 128 MiB of HBM per device.

v0:
```python
import jax
import jax.numpy as jnp
from jax import lax
from jax.sharding import Mesh
from jax.sharding import PartitionSpec as P

ROWS = ("rows_0", "rows_1")
ROWS_WIDTH = ("rows_0", "rows_1", "width_0", "width_1")
SITE_ROWS = ("site", "rows_0", "rows_1")
WIDTH = ("width_0", "width_1")
SITE_ROWS_WIDTH = ("site", "rows_0", "rows_1", "width_0", "width_1")
SITE_WIDTH = ("site", "width_0", "width_1")


def copy_for_each(array, axis):
    copies = jnp.broadcast_to(array, (lax.axis_size(axis), *array.shape))
    return lax.all_to_all(copies, axis, split_axis=0, concat_axis=0, tiled=True)


def of_everyone(array, axis):
    return copy_for_each(array, axis).max(axis=0)


def packed_total(arrays, axis):
    ends = [0]
    for a in arrays:
        ends.append(ends[-1] + a.size)
    so_far = of_everyone(jnp.concatenate([a.ravel() for a in arrays]), axis)
    return tuple((so_far[b:e].reshape(a.shape) for a, b, e in zip(arrays, ends, ends[1:])))


def in_one_piece(arrays, axis, dim, along):
    both = jnp.concatenate(arrays, axis=along)
    whole, at, finished = (lax.all_gather(both, axis, axis=dim, tiled=True), 0, [])
    for a in arrays:
        finished.append(lax.slice_in_dim(whole, at, at + a.shape[along], axis=along))
        at += a.shape[along]
    return tuple(finished)


def joined_along(blocks, dim):
    lengths = list(blocks.shape[1:])
    lengths[dim] *= blocks.shape[0]
    return jnp.moveaxis(blocks, 0, dim).reshape(lengths)


def stacked_from(array, axes, turns):
    blocks = array
    for k in turns:
        blocks = lax.all_gather(blocks, axes[k])
    done = turns[::-1]
    back = [done.index(k) for k in range(len(axes))]
    blocks = blocks.transpose(*back, *range(len(axes), blocks.ndim))
    return blocks.reshape(-1, *array.shape)


def whole_of(array, axes, turns, dim):
    return joined_along(stacked_from(array, axes, turns), dim)


def shards(
    one_query,
    other_query,
    one_key,
    other_key,
    one_value,
    other_value,
    mix_share,
    norm_train,
    norm_step,
):
    whole_query = mix_share[:, None] * one_query + (1.0 - mix_share[:, None]) * other_query
    whole_key = mix_share[:, None] * one_key + (1.0 - mix_share[:, None]) * other_key
    whole_value = mix_share[:, None] * one_value + (1.0 - mix_share[:, None]) * other_value
    scale_query, scale_key, scale_value = packed_total(
        (
            jnp.max(jnp.abs(whole_query), axis=0),
            jnp.max(jnp.abs(whole_key), axis=0),
            jnp.max(jnp.abs(whole_value), axis=0),
        ),
        ROWS,
    )
    narrow_query, narrow_key, narrow_value = (
        (whole_query / scale_query).astype(jnp.bfloat16),
        (whole_key / scale_key).astype(jnp.bfloat16),
        (whole_value / scale_value).astype(jnp.bfloat16),
    )
    serving_query, serving_key, serving_value = in_one_piece(
        (narrow_query, narrow_key, narrow_value), ROWS, 0, 1
    )
    serve_norm = whole_of(
        (norm_train + norm_step).astype(jnp.bfloat16), ROWS_WIDTH, (2, 0, 3, 1), 0
    )
    return (
        serving_query,
        serving_key,
        serving_value,
        scale_query,
        scale_key,
        scale_value,
        serve_norm,
    )


def solution(mesh):
    split = Mesh(
        mesh.devices.reshape(mesh.shape["site"], 8, 2, 2, 4),
        ("site", "rows_0", "rows_1", "width_0", "width_1"),
    )
    return jax.shard_map(
        shards,
        mesh=split,
        in_specs=(
            P(SITE_ROWS, WIDTH),
            P(SITE_ROWS, WIDTH),
            P(SITE_ROWS, WIDTH),
            P(SITE_ROWS, WIDTH),
            P(SITE_ROWS, WIDTH),
            P(SITE_ROWS, WIDTH),
            P(SITE_ROWS),
            P(SITE_ROWS_WIDTH),
            P(SITE_ROWS_WIDTH),
        ),
        out_specs=(
            P("site", WIDTH),
            P("site", WIDTH),
            P("site", WIDTH),
            P(SITE_WIDTH),
            P(SITE_WIDTH),
            P(SITE_WIDTH),
            P("site"),
        ),
        check_vma=False,
    )
```

profile of v0, /device:TPU:1, one launch (start us, length us, event | category | flops | bytes accessed | tf_op | source)
XLA Modules:
  0.0 145.0 jit_solution(4714112330016848287)
XLA Ops:
  7.2 0.0 all-gather.7.cloned.1.call-start
  7.2 0.7 broadcast_subtract_fusion
  7.9 0.0 copy-start.6
  7.9 0.0 copy-start
  7.9 0.0 copy-start.1
  7.9 2.3 %abs_reduce_fusion = f32[896]{0:T(1024)S(1)} fusion(f32[448,896]{1,0:T(8,128)} %param.10, f32[448]{0:T(512)S(1)} %broadcast_subtract_fusion, f32[448,896]{1,0:T(8,128)} %param.9, f32[448]{0:T(512)} %param.15), kind=kLoop, calls=%fused_computation.1 | loop fusion | flops 2006144 | bytes 3218432 | tf_op jit(solution)/shard_map/reduce_max | solution.py:77
  10.2 0.0 copy-done.6
  10.2 1.5 %abs_reduce_fusion.2 = (f32[128]{0:T(128)S(1)}, f32[128]{0:T(128)S(1)}) fusion(f32[448,128]{1,0:T(8,128)} %param.12, f32[448]{0:T(512)S(1)} %broadcast_subtract_fusion, f32[448,128]{1,0:T(8,128)} %param.11, f32[448]{0:T(512)S(1)} %copy-done.6, f32[448,128]{1,0:T(8,128)} %param.14, f32[448,128]{1,0:T(8,128)} %param.13), kind=kLoop, calls=%fused_computation.8 | loop fusion | flops 573184 | bytes 922112 | tf_op jit(solution)/shard_map/reduce_max | solution.py:78
  11.8 17.7 %all_to_all.6 = f32[16,1,1152]{2,1,0:T(1,128)S(1)} all-to-all(f32[16,1,1152]{2,1,0:T(1,128)S(1)} %broadcast_in_dim.2), channel_id=1, replica_groups=mesh['site'=2,'rows_0'=8,'rows_1'=2,'width_0'=2,'width_1'=4] {'rows_0','..., dimensions={0} | all-to-all | bytes 147456 | tf_op jit(solution)/shard_map/all_to_all | solution.py:17
  29.5 0.1 reduce_max.39
  29.6 0.0 copy-start.8
  29.6 0.0 copy-start.9
  29.6 0.0 copy-done
  29.6 0.0 copy-done.1
  29.6 0.0 copy-start.7
  29.6 0.0 copy-start.2
  29.6 0.0 copy-start.3
  29.7 0.0 copy-start.4
  29.7 0.0 copy-start.5
  29.7 0.3 divide_convert_fusion
  30.0 0.2 copy-done.7
  30.2 0.0 copy-done.8
  30.2 0.0 copy-done.9
  30.2 0.4 copy-done.2
  30.6 0.1 copy-done.3
  30.7 0.1 copy-done.4
  30.8 0.1 copy-done.5
  30.9 0.2 divide_convert_fusion.2
  31.1 0.0 copy-start.12
  31.1 0.0 copy-start.10
  31.1 0.0 copy-start.11
  31.2 1.1 pad_maximum_fusion
  32.2 0.0 all-gather.7.cloned.1.call-update
  32.2 0.0 copy-done.12
  32.2 0.6 dynamic-slice
  33.5 0.0 copy-done.10
  33.5 0.0 copy-done.11
  33.5 0.2 dynamic-update-slice
  33.8 5.3 %all-reduce = bf16[112]{0:T(256)(128)(2,1)S(1)} all-reduce(bf16[112]{0:T(256)(128)(2,1)S(1)} %dynamic-update-slice), channel_id=2, replica_groups=mesh['site'=2,'rows_0'=8,'rows_1'=2,'width_0'=2,'width_1'=4] {'width_0'}, use_global_device_ids=true, to_apply=%add | all-reduce | flops 112 | bytes 448
  39.0 0.1 reshape.31
  39.1 11.5 %all-gather.4 = bf16[8,2,56]{2,1,0:T(2,128)(2,1)S(1)} all-gather(bf16[1,2,56]{2,1,0:T(2,128)(2,1)S(1)} %reshape.31), channel_id=3, replica_groups=mesh['site'=2,'rows_0'=8,'rows_1'=2,'width_0'=2,'width_1'=4] {'rows_0'}, dimensions={0}, use_global_device_ids=true | all-gather | bytes 2016 | tf_op jit(solution)/shard_map/all_gather | solution.py:50
  50.6 10.4 %all-gather.2 = bf16[32,2,56]{2,1,0:T(2,128)(2,1)S(1)} all-gather(bf16[8,2,56]{2,1,0:T(2,128)(2,1)S(1)} %all-gather.4), channel_id=4, replica_groups=mesh['site'=2,'rows_0'=8,'rows_1'=2,'width_0'=2,'width_1'=4] {'width_1'}, dimensions={0}, use_global_device_ids=true | all-gather | bytes 8960 | tf_op jit(solution)/shard_map/all_gather | solution.py:50
  61.0 7.5 %all-gather.3 = bf16[8,8,2,56]{3,1,2,0:T(8,128)(2,1)S(1)} all-gather(bf16[4,8,2,56]{3,1,2,0:T(8,128)(2,1)S(1)} %copy.23), channel_id=5, replica_groups=mesh['site'=2,'rows_0'=8,'rows_1'=2,'width_0'=2,'width_1'=4] {'rows_1'}, dimensions={0}, use_global_device_ids=true | all-gather | bytes 21504 | tf_op jit(solution)/shard_map/all_gather | solution.py:50
  68.5 0.7 reshape_reshape.3
  69.2 54.1 %all-gather.7.cloned.1.call-done = bf16[7168,1152]{1,0:T(8,128)(2,1)} async-done(((bf16[448,1152]{1,0:T(8,128)(2,1)}), bf16[7168,1152]{1,0:T(8,128)(2,1)}) %all-gather.7.cloned.1.call-update) | async-done | bytes 16515088 | tf_op jit(solution)/shard_map/all_gather | solution.py:34
  123.4 10.7 %slice.27 = bf16[7168,896]{1,0:T(8,128)(2,1)} slice(bf16[7168,1152]{1,0:T(8,128)(2,1)} %all-gather.7.cloned.1.call-done), slice={[0:7168], [0:896]} | slice | bytes 25690112 | tf_op jit(solution)/shard_map/slice | solution.py:36
  134.0 4.1 %fusion = (bf16[7168,128]{1,0:T(8,128)(2,1)}, bf16[7168,128]{1,0:T(8,128)(2,1)}) fusion(bf16[7168,1152]{1,0:T(8,128)(2,1)} %all-gather.7.cloned.1.call-done), kind=kLoop, calls=%fused_computation.13 | loop fusion | bytes 7340032 | tf_op jit(solution)/shard_map/slice | solution.py:36
  (8 shorter events, 0.1 us)
Async XLA Ops:
  7.2 116.2 %all-gather.7.cloned.1.call-start = ((), (), s32[]{:S(2)}) async-start(), calls=%async_computation.1 | async-start | bytes 17547264 | tf_op jit(solution)/shard_map/all_gather | solution.py:34
  7.9 2.3 %copy-start.6 = (f32[448]{0:T(512)S(1)}, f32[448]{0:T(512)}, u32[]{:S(2)}) copy-start(f32[448]{0:T(512)} %param.15) | copy-start | bytes 5380
  7.9 21.7 %copy-start = (f32[448,896]{1,0:T(8,128)S(1)}, f32[448,896]{1,0:T(8,128)}, u32[]{:S(2)}) copy-start(f32[448,896]{1,0:T(8,128)} %param.10) | copy-start | bytes 4816900
  7.9 21.7 %copy-start.1 = (f32[448,896]{1,0:T(8,128)S(1)}, f32[448,896]{1,0:T(8,128)}, u32[]{:S(2)}) copy-start(f32[448,896]{1,0:T(8,128)} %param.9) | copy-start | bytes 4816900
  29.6 0.7 copy-start.8
  29.6 0.6 copy-start.9
  29.6 0.6 copy-start.7
  29.6 0.9 copy-start.2
  29.6 1.0 copy-start.3
  29.7 1.1 copy-start.4
  29.7 1.3 copy-start.5
  31.1 1.1 copy-start.12
  31.1 2.4 %copy-start.10 = (f32[56]{0:T(128)S(1)}, f32[56]{0:T(128)}, u32[]{:S(2)}) copy-start(f32[56]{0:T(128)} %param.16) | copy-start | bytes 676
  31.1 2.4 %copy-start.11 = (f32[56]{0:T(128)S(1)}, f32[56]{0:T(128)}, u32[]{:S(2)}) copy-start(f32[56]{0:T(128)} %param.17) | copy-start | bytes 676
Sparse Core Ops, SparseCore 0:
  32.4 90.9 all-gather.6
where the time goes:
time: 145 us
  waiting for transfers between devices  54.1 us (37%)
  blocking collectives  52.3 us (36%)
  local copies, waits for them, and re-layouts  17.5 us (12%)
  between operations  14.9 us (10%)
  other arithmetic  6.11 us (4%)
    all_gather x1, waiting for transfers between devices, in_one_piece(): lax.all_gather(both, axis, axis=dim, tiled=True)  54.1 us
    all_gather x3, blocking collectives, stacked_from(): blocks = lax.all_gather(blocks, axes[k])  29.4 us
    all_to_all x1, blocking collectives, copy_for_each(): return lax.all_to_all(copies, axis, split_axis=0, concat_axis=0, tiled=True)  17.7 us
    slice x2, local copies, waits for them, and re-layouts, in_one_piece(): lax.slice_in_dim(whole, at, at + a.shape[along], axis=along)  14.8 us
    unnamed x1, blocking collectives  5.26 us
  transfers between devices with their start and end apart: 1, of which 1 were waited for; matrix products, arithmetic and copies ran while one was open for 1% of the time, Pallas kernels for 0%

commit v1 on v0

v1 whole, which is shorter than its diff:
```python
import jax
import jax.numpy as jnp
from jax import lax
from jax.experimental import pallas as pl
from jax.sharding import PartitionSpec as P

SITE_ROWS = ("site", "rows")
SITE_ROWS_WIDTH = ("site", "rows", "width")
SITE_WIDTH = ("site", "width")


def left_open(*shapes):
    return pl.pallas_call(
        lambda *refs: None,
        out_shape=tuple(jax.ShapeDtypeStruct(s, jnp.bfloat16) for s in shapes),
        out_specs=tuple(pl.BlockSpec(memory_space=pl.ANY) for s in shapes),
    )()


def partner(array):
    n = lax.axis_size("rows")
    return lax.ppermute(array, "rows", [(i, i ^ 1) for i in range(n)])


def onward(array):
    n = lax.axis_size("rows")

    def to(i):
        return (i + 2) % n if i % 2 == 0 else (i - 2) % n

    return lax.ppermute(array, "rows", [(i, to(i)) for i in range(n)])


def body(
    one_query, other_query, one_key, other_key, one_value, other_value, mix_share, norm_train, norm_step):
    n = lax.axis_size("rows")
    wide = lax.axis_size("width")
    me = lax.axis_index("rows")
    core = me & 1
    share = mix_share[:, None]
    rest = 1.0 - share
    wholes = [
        share * one + rest * other
        for one, other in ((one_query, other_query), (one_key, other_key), (one_value, other_value))
    ]
    widths = [a.shape[1] for a in wholes]
    ends = [0, widths[0], widths[0] + widths[1], sum(widths)]
    norm = (norm_train + norm_step).astype(jnp.bfloat16)
    own = jnp.concatenate([jnp.max(jnp.abs(a), axis=0) for a in wholes] + [norm.astype(jnp.float32)])
    seen = lax.all_to_all(
        jnp.broadcast_to(own, (n, own.shape[0])), "rows", split_axis=0, concat_axis=0, tiled=True
    )
    tops = seen.max(axis=0)
    scales = [tops[b:e] for b, e in zip(ends, ends[1:])]
    norms = seen[:, ends[3] :].astype(jnp.bfloat16)

    depth = one_query.shape[0]
    mine = jnp.concatenate([(a / s).astype(jnp.bfloat16) for a, s in zip(wholes, scales)], axis=1)
    outs = left_open(*[(n * depth, w) for w in widths])

    def put(outs, block, owner):
        at = (owner * depth).astype(jnp.int32)
        return [
            lax.dynamic_update_slice(out, block[:, b:e], (at, jnp.int32(0)), allow_negative_indices=False)
            for out, b, e in zip(outs, ends, ends[1:])
        ]

    ahead = 2 - 4 * core

    def chip(hops, of):
        return ((me - core - ahead * hops) & (n - 1)) + of

    own, other = core, core ^ 1
    sibling = partner(mine)
    units = [mine, sibling]
    half = n // 4
    outs = put(outs, mine, me)
    outs = put(outs, sibling, me ^ 1)
    for step in range(1, 2 * half):
        hop, chain = (step + 1) // 2, (step + 1) % 2
        here = onward(units[step - 1])
        units.append(here)
        outs = put(outs, here, chip(hop, core ^ chain))
        across = partner(here)
        outs = put(outs, across, chip(-hop, core ^ 1 ^ chain))

    k = 1
    while k < wide:
        other = lax.ppermute(norms, "width", [(i, i ^ k) for i in range(wide)])
        low = (lax.axis_index("width") & k) == 0
        a, b = jnp.where(low, norms, other), jnp.where(low, other, norms)
        norms = jnp.concatenate([a[:, None], b[:, None]], axis=1).reshape(n, -1)
        k *= 2
    return (*outs, *scales, norms.reshape(-1))


def solution(mesh):
    return jax.shard_map(
        body,
        mesh=mesh,
        in_specs=(P(SITE_ROWS, "width"),) * 6 + (P(SITE_ROWS), P(SITE_ROWS_WIDTH), P(SITE_ROWS_WIDTH)),
        out_specs=(P("site", "width"),) * 3 + (P(SITE_WIDTH),) * 3 + (P("site"),),
        check_vma=False,
    )
```

time: 145 us -> 136 us (0.938)
  blocking collectives: 52.3 us -> 0 us
  starting transfers between devices: 0.04 us -> 49.8 us
  between operations: 14.9 us -> 0.89 us
  local copies, waits for them, and re-layouts: 17.5 us -> 30.6 us
  waiting for transfers between devices: 54.1 us -> 46.9 us
    all_gather x1 -> x0, waiting for transfers between devices: 54.1 us -> none  [in_one_piece(): lax.all_gather(both, axis, axis=dim, tiled=True)]
    ppermute x0 -> x18, starting transfers between devices: none -> 39.8 us  [the longest x8 21.2 us: partner(): return lax.ppermute(array, 'rows', [(i, i ^ 1) for i in range(n)])]
    ppermute x0 -> x18, waiting for transfers between devices: none -> 38.8 us  [the longest x7 36.3 us: onward(): return lax.ppermute(array, 'rows', [(i, to(i)) for i in range(n)])]
    all_gather x3 -> x0, blocking collectives: 29.4 us -> none  [stacked_from(): blocks = lax.all_gather(blocks, axes[k])]
    dynamic_update_slice x0 -> x30, local copies, waits for them, and re-layouts: none -> 28.9 us  [put(): lax.dynamic_update_slice(out, block[:, b:e], (at, jnp.int32(0)), allow_ne...]
    all_to_all x1 -> x0, blocking collectives: 17.7 us -> none  [copy_for_each(): return lax.all_to_all(copies, axis, split_axis=0, concat_axis=0, tiled=True)]
    slice x4 -> x3, local copies, waits for them, and re-layouts: 14.8 us -> 0.01 us  [the longest x2 0.01 us: body(): scales = [tops[b:e] for b, e in zip(ends, ends[1:])]]
    all_to_all x0 -> x1, starting transfers between devices: none -> 9.97 us  [body(): lax.all_to_all(jnp.broadcast_to(own, (n, own.shape[0])), 'rows', split_ax...]
  transfers between devices with their start and end apart: 1 -> 19, of which waited for: 1 -> 7; matrix products, arithmetic and copies ran while one was open for 1% -> 21% of each run, Pallas kernels for 0% -> 0%
where the time goes in v1:
time: 136 us; the launch traced here: 135 us
  starting transfers between devices  49.8 us (37%)
  waiting for transfers between devices  46.9 us (34%)
  local copies, waits for them, and re-layouts  30.6 us (22%)
  other arithmetic  7.26 us (5%)
    ppermute x7, waiting for transfers between devices, onward(): return lax.ppermute(array, 'rows', [(i, to(i)) for i in range(n)])  36.3 us
    dynamic_update_slice x30, local copies, waits for them, and re-layouts, put(): lax.dynamic_update_slice(out, block[:, b:e], (at, jnp.int32(0)), allow_ne...  28.9 us
    ppermute x8, starting transfers between devices, partner(): return lax.ppermute(array, 'rows', [(i, i ^ 1) for i in range(n)])  21.2 us
    ppermute x7, starting transfers between devices, onward(): return lax.ppermute(array, 'rows', [(i, to(i)) for i in range(n)])  11.7 us
    all_to_all x1, starting transfers between devices, body(): lax.all_to_all(jnp.broadcast_to(own, (n, own.shape[0])), 'rows', split_ax...  9.97 us
    all_to_all x1, waiting for transfers between devices, body(): lax.all_to_all(jnp.broadcast_to(own, (n, own.shape[0])), 'rows', split_ax...  8.1 us
    ppermute x3, starting transfers between devices, body(): other = lax.ppermute(norms, 'width', [(i, i ^ k) for i in range(wide)])  6.99 us
  transfers between devices with their start and end apart: 19, of which 7 were waited for; matrix products, arithmetic and copies ran while one was open for 21% of the time, Pallas kernels for 0%

profile of v1, /device:TPU:1, one launch (start us, length us, event | category | flops | bytes accessed | tf_op | source)
XLA Modules:
  0.0 135.5 jit_solution(2987109009347098122)
XLA Ops:
  0.7 0.8 broadcast_subtract_fusion
  2.1 2.3 %abs_reduce_fusion = f32[896]{0:T(1024)S(1)} fusion(f32[448,896]{1,0:T(8,128)} %param.10, f32[448]{0:T(512)S(1)} %broadcast_subtract_fusion, f32[448,896]{1,0:T(8,128)} %param.9, f32[448]{0:T(512)} %param.15), kind=kLoop, calls=%fused_computation.1 | loop fusion | flops 2006144 | bytes 3218432 | tf_op jit(solution)/shard_map/reduce_max | solution.py:49
  5.4 10.0 %all-to-all-start = ((f32[16,1,1208]{2,1,0:T(1,128)}), f32[16,1,1208]{2,1,0:T(1,128)S(1)}, u32[]{:S(2)}, u32[]{:S(2)}) async-start(f32[16,1,1208]{2,1,0:T(1,128)} %broadcast_in_dim.25), calls=%async_computation | async-start | bytes 163840 | tf_op jit(solution)/shard_map/all_to_all | solution.py:50
  15.4 8.1 %all-to-all-done = f32[16,1,1208]{2,1,0:T(1,128)S(1)} async-done(((f32[16,1,1208]{2,1,0:T(1,128)}), f32[16,1,1208]{2,1,0:T(1,128)S(1)}, u32[]{:S(2)}, u32[]{:S(2)}) %all-to-all-start) | async-done | bytes 77344 | tf_op jit(solution)/shard_map/all_to_all | solution.py:50
  23.7 1.2 constant_dynamic-update-slice_fusion.2
  24.9 0.9 constant_dynamic-update-slice_fusion.1
  25.8 1.1 pad_maximum_fusion
  27.4 1.3 collective-permute-start.15
  28.6 1.2 collective-permute-done.15
  30.0 2.8 %collective-permute-start.16 = (bf16[16,112]{1,0:T(8,128)(2,1)S(1)}, bf16[16,112]{1,0:T(8,128)(2,1)S(1)}, u32[]{:S(2)}, u32[]{:S(2)}) collective-permute-start(bf16[16,112]{1,0:T(8,128)(2,1)S(1)} %reshape.31), channel_id=1, source_target_pairs={{0,2},{1,3},{2,0},{3,1},{4,6},{5,7},{6,4},{7,5},{8,10},{9,11},{10,... | collective-permute-start | bytes 10760 | tf_op jit(solution)/shard_map/ppermute | solution.py:89
  32.8 1.2 collective-permute-done.16
  34.1 2.9 %collective-permute-start.17 = (bf16[16,224]{1,0:T(8,128)(2,1)S(1)}, bf16[16,224]{1,0:T(8,128)(2,1)S(1)}, u32[]{:S(2)}, u32[]{:S(2)}) collective-permute-start(bf16[16,224]{1,0:T(8,128)(2,1)S(1)} %reshape.32), channel_id=1, source_target_pairs={{0,4},{1,5},{2,6},{3,7},{4,0},{5,1},{6,2},{7,3},{8,12},{9,13},{10,... | collective-permute-start | bytes 21512 | tf_op jit(solution)/shard_map/ppermute | solution.py:89
  37.0 3.8 %collective-permute-done.1 = bf16[448,1152]{1,0:T(8,128)(2,1)S(1)} collective-permute-done((bf16[448,1152]{1,0:T(8,128)(2,1)}, bf16[448,1152]{1,0:T(8,128)(2,1)S(1)}, u32[]{:S(2)}, u32[]{:S(2)}) %collective-permute-start.1) | collective-permute-done | bytes 1032224 | tf_op jit(solution)/shard_map/ppermute | solution.py:31
  40.9 1.0 collective-permute-start.5
  41.9 1.3 collective-permute-start.2
  43.2 0.7 reshape_reshape.3
  44.6 0.9 slice_dynamic-update-slice_fusion.14
  45.5 0.9 slice_dynamic-update-slice_fusion.13
  46.5 19.3 %collective-permute-done.3 = bf16[448,1152]{1,0:T(8,128)(2,1)} collective-permute-done((bf16[448,1152]{1,0:T(8,128)(2,1)S(1)}, bf16[448,1152]{1,0:T(8,128)(2,1)}, u32[]{:S(2)}, u32[]{:S(2)}) %collective-permute-start.3) | collective-permute-done | bytes 1032224 | tf_op jit(solution)/shard_map/ppermute | solution.py:31
  65.8 1.9 %collective-permute-start.7 = (bf16[448,1152]{1,0:T(8,128)(2,1)}, bf16[448,1152]{1,0:T(8,128)(2,1)S(1)}, u32[]{:S(2)}, u32[]{:S(2)}) collective-permute-start(bf16[448,1152]{1,0:T(8,128)(2,1)} %collective-permute-done.3), channel_id=1, source_target_pairs={{0,16},{8,120},{16,32},{24,8},{32,48},{40,24},{48,64},{56,40},{64,... | collective-permute-start | bytes 3096584 | tf_op jit(solution)/shard_map/ppermute | solution.py:31
  67.7 2.2 %collective-permute-start.4 = (bf16[448,1152]{1,0:T(8,128)(2,1)}, bf16[448,1152]{1,0:T(8,128)(2,1)S(1)}, u32[]{:S(2)}, u32[]{:S(2)}) collective-permute-start(bf16[448,1152]{1,0:T(8,128)(2,1)} %collective-permute-done.3), channel_id=1, source_target_pairs={{0,8},{8,0},{16,24},{24,16},{32,40},{40,32},{48,56},{56,48},{64,72... | collective-permute-start | bytes 3096584 | tf_op jit(solution)/shard_map/ppermute | solution.py:22
  69.9 3.0 %collective-permute-start.9 = (bf16[448,1152]{1,0:T(8,128)(2,1)S(1)}, bf16[448,1152]{1,0:T(8,128)(2,1)S(1)}, u32[]{:S(2)}, u32[]{:S(2)}) collective-permute-start(bf16[448,1152]{1,0:T(8,128)(2,1)S(1)} %collective-permute-done.5), channel_id=1, source_target_pairs={{0,16},{8,120},{16,32},{24,8},{32,48},{40,24},{48,64},{56,40},{64,... | collective-permute-start | bytes 3096584 | tf_op jit(solution)/shard_map/ppermute | solution.py:31
  73.6 1.7 %slice_dynamic-update-slice_fusion.27 = (bf16[7168,128]{1,0:T(8,128)(2,1)}, bf16[7168,128]{1,0:T(8,128)(2,1)}) fusion(bf16[7168,128]{1,0:T(8,128)(2,1)} %get-tuple-element.47, s32[]{:T(128)S(6)} %mul.136, bf16[448,1152]{1,0:T(8,128)(2,1)} %collective-permute-done.2, bf16[7168,128]{1,0:T(8,128)(2,1)} %get-tuple-element.48), kind=kLoop, calls=%fused_computation.37 | loop fusion | bytes 458756 | tf_op jit(solution)/shard_map/dynamic_update_slice | solution.py:64
  75.2 2.1 %slice_dynamic-update-slice_fusion.12 = bf16[7168,896]{1,0:T(8,128)(2,1)} fusion(bf16[7168,896]{1,0:T(8,128)(2,1)} %slice_dynamic-update-slice_fusion.13, s32[]{:T(128)S(6)} %mul.136, bf16[448,1152]{1,0:T(8,128)(2,1)} %collective-permute-done.2), kind=kLoop, calls=%fused_computation.16 | loop fusion | bytes 1605636 | tf_op jit(solution)/shard_map/dynamic_update_slice | solution.py:64
  77.3 1.7 %slice_dynamic-update-slice_fusion.26 = (bf16[7168,128]{1,0:T(8,128)(2,1)}, bf16[7168,128]{1,0:T(8,128)(2,1)}) fusion(bf16[7168,128]{1,0:T(8,128)(2,1)} %get-tuple-element.45, s32[]{:T(128)S(6)} %mul.137, bf16[448,1152]{1,0:T(8,128)(2,1)} %collective-permute-done.3, bf16[7168,128]{1,0:T(8,128)(2,1)} %get-tuple-element.46), kind=kLoop, calls=%fused_computation.36 | loop fusion | bytes 458756 | tf_op jit(solution)/shard_map/dynamic_update_slice | solution.py:64
  79.0 2.1 %slice_dynamic-update-slice_fusion.11 = bf16[7168,896]{1,0:T(8,128)(2,1)} fusion(bf16[7168,896]{1,0:T(8,128)(2,1)} %slice_dynamic-update-slice_fusion.12, s32[]{:T(128)S(6)} %mul.137, bf16[448,1152]{1,0:T(8,128)(2,1)} %collective-permute-done.3), kind=kLoop, calls=%fused_computation.15 | loop fusion | bytes 1605636 | tf_op jit(solution)/shard_map/dynamic_update_slice | solution.py:64
  81.1 9.8 %collective-permute-done.9 = bf16[448,1152]{1,0:T(8,128)(2,1)S(1)} collective-permute-done((bf16[448,1152]{1,0:T(8,128)(2,1)S(1)}, bf16[448,1152]{1,0:T(8,128)(2,1)S(1)}, u32[]{:S(2)}, u32[]{:S(2)}) %collective-permute-start.9) | collective-permute-done | bytes 1032224 | tf_op jit(solution)/shard_map/ppermute | solution.py:31
  90.8 2.8 %collective-permute-start.13 = (bf16[448,1152]{1,0:T(8,128)(2,1)S(1)}, bf16[448,1152]{1,0:T(8,128)(2,1)S(1)}, u32[]{:S(2)}, u32[]{:S(2)}) collective-permute-start(bf16[448,1152]{1,0:T(8,128)(2,1)S(1)} %collective-permute-done.9), channel_id=1, source_target_pairs={{0,16},{8,120},{16,32},{24,8},{32,48},{40,24},{48,64},{56,40},{64,... | collective-permute-start | bytes 3096584 | tf_op jit(solution)/shard_map/ppermute | solution.py:31
  93.6 3.4 %collective-permute-start.10 = (bf16[448,1152]{1,0:T(8,128)(2,1)S(1)}, bf16[448,1152]{1,0:T(8,128)(2,1)S(1)}, u32[]{:S(2)}, u32[]{:S(2)}) collective-permute-start(bf16[448,1152]{1,0:T(8,128)(2,1)S(1)} %collective-permute-done.9), channel_id=1, source_target_pairs={{0,8},{8,0},{16,24},{24,16},{32,40},{40,32},{48,56},{56,48},{64,72... | collective-permute-start | bytes 3096584 | tf_op jit(solution)/shard_map/ppermute | solution.py:22
  97.0 3.0 %collective-permute-start.11 = (bf16[448,1152]{1,0:T(8,128)(2,1)S(1)}, bf16[448,1152]{1,0:T(8,128)(2,1)S(1)}, u32[]{:S(2)}, u32[]{:S(2)}) collective-permute-start(bf16[448,1152]{1,0:T(8,128)(2,1)S(1)} %collective-permute-done.7), channel_id=1, source_target_pairs={{0,16},{8,120},{16,32},{24,8},{32,48},{40,24},{48,64},{56,40},{64,... | collective-permute-start | bytes 3096584 | tf_op jit(solution)/shard_map/ppermute | solution.py:31
  100.0 0.7 slice_dynamic-update-slice_fusion.25
  101.4 0.9 slice_dynamic-update-slice_fusion.10
  102.3 0.7 slice_dynamic-update-slice_fusion.23
  103.0 0.9 slice_dynamic-update-slice_fusion.9
  104.0 0.9 slice_dynamic-update-slice_fusion.8
  105.6 0.9 slice_dynamic-update-slice_fusion.7
  106.6 6.3 %collective-permute-start.14 = (bf16[448,1152]{1,0:T(8,128)(2,1)S(1)}, bf16[448,1152]{1,0:T(8,128)(2,1)S(1)}, u32[]{:S(2)}, u32[]{:S(2)}) collective-permute-start(bf16[448,1152]{1,0:T(8,128)(2,1)S(1)} %collective-permute-done.13), channel_id=1, source_target_pairs={{0,8},{8,0},{16,24},{24,16},{32,40},{40,32},{48,56},{56,48},{64,72... | collective-permute-start | bytes 3096584 | tf_op jit(solution)/shard_map/ppermute | solution.py:22
  112.9 3.4 %collective-permute-done.11 = bf16[448,1152]{1,0:T(8,128)(2,1)S(1)} collective-permute-done((bf16[448,1152]{1,0:T(8,128)(2,1)S(1)}, bf16[448,1152]{1,0:T(8,128)(2,1)S(1)}, u32[]{:S(2)}, u32[]{:S(2)}) %collective-permute-start.11) | collective-permute-done | bytes 1032224 | tf_op jit(solution)/shard_map/ppermute | solution.py:31
  116.3 7.6 %collective-permute-start.12 = (bf16[448,1152]{1,0:T(8,128)(2,1)S(1)}, bf16[448,1152]{1,0:T(8,128)(2,1)S(1)}, u32[]{:S(2)}, u32[]{:S(2)}) collective-permute-start(bf16[448,1152]{1,0:T(8,128)(2,1)S(1)} %collective-permute-done.11), channel_id=1, source_target_pairs={{0,8},{8,0},{16,24},{24,16},{32,40},{40,32},{48,56},{56,48},{64,72... | collective-permute-start | bytes 3096584 | tf_op jit(solution)/shard_map/ppermute | solution.py:22
  123.9 0.7 slice_dynamic-update-slice_fusion.21
  125.3 0.9 slice_dynamic-update-slice_fusion.6
  127.0 0.9 slice_dynamic-update-slice_fusion.5
  127.9 0.9 slice_dynamic-update-slice_fusion.4
  128.9 0.9 slice_dynamic-update-slice_fusion.3
  130.5 0.7 slice_dynamic-update-slice_fusion.17
  131.9 0.9 slice_dynamic-update-slice_fusion.2
  132.9 0.9 slice_dynamic-update-slice_fusion.1
  133.8 0.9 slice_dynamic-update-slice_fusion
  (73 shorter events, 8.8 us)
Async XLA Ops:
  0.6 3.8 %copy-start.9 = (f32[448]{0:T(512)S(1)}, f32[448]{0:T(512)}, u32[]{:S(2)}) copy-start(f32[448]{0:T(512)} %param.15) | copy-start | bytes 5380
  0.6 3.8 %copy-start.5 = (f32[448,128]{1,0:T(8,128)S(1)}, f32[448,128]{1,0:T(8,128)}, u32[]{:S(2)}) copy-start(f32[448,128]{1,0:T(8,128)} %param.14) | copy-start | bytes 688132
  0.7 3.8 %copy-start.7 = (f32[448,128]{1,0:T(8,128)S(1)}, f32[448,128]{1,0:T(8,128)}, u32[]{:S(2)}) copy-start(f32[448,128]{1,0:T(8,128)} %param.13) | copy-start | bytes 688132
  0.7 3.8 %copy-start.2 = (f32[448,128]{1,0:T(8,128)S(1)}, f32[448,128]{1,0:T(8,128)}, u32[]{:S(2)}) copy-start(f32[448,128]{1,0:T(8,128)} %param.12) | copy-start | bytes 688132
  0.7 3.8 %copy-start.3 = (f32[448,128]{1,0:T(8,128)S(1)}, f32[448,128]{1,0:T(8,128)}, u32[]{:S(2)}) copy-start(f32[448,128]{1,0:T(8,128)} %param.11) | copy-start | bytes 688132
  2.1 21.5 %copy-start = (f32[448,896]{1,0:T(8,128)S(1)}, f32[448,896]{1,0:T(8,128)}, u32[]{:S(2)}) copy-start(f32[448,896]{1,0:T(8,128)} %param.10) | copy-start | bytes 4816900
  2.1 21.5 %copy-start.1 = (f32[448,896]{1,0:T(8,128)S(1)}, f32[448,896]{1,0:T(8,128)}, u32[]{:S(2)}) copy-start(f32[448,896]{1,0:T(8,128)} %param.9) | copy-start | bytes 4816900
  5.4 18.1 %all-to-all-start = ((f32[16,1,1208]{2,1,0:T(1,128)}), f32[16,1,1208]{2,1,0:T(1,128)S(1)}, u32[]{:S(2)}, u32[]{:S(2)}) async-start(f32[16,1,1208]{2,1,0:T(1,128)} %broadcast_in_dim.25), calls=%async_computation | async-start | bytes 163840 | tf_op jit(solution)/shard_map/all_to_all | solution.py:50
  23.6 1.3 copy-start.11
  23.6 1.3 copy-start.12
  23.6 1.3 copy-start.10
  23.6 1.3 copy-start.4
  23.6 1.3 copy-start.6
  23.7 1.3 copy-start.8
  26.9 14.0 %collective-permute-start.1 = (bf16[448,1152]{1,0:T(8,128)(2,1)}, bf16[448,1152]{1,0:T(8,128)(2,1)S(1)}, u32[]{:S(2)}, u32[]{:S(2)}) collective-permute-start(bf16[448,1152]{1,0:T(8,128)(2,1)} %pad_maximum_fusion), channel_id=1, source_target_pairs={{0,16},{8,120},{16,32},{24,8},{32,48},{40,24},{48,64},{56,40},{64,... | collective-permute-start | bytes 3096584 | tf_op jit(solution)/shard_map/ppermute | solution.py:31
  26.9 14.9 %collective-permute-start = (bf16[448,1152]{1,0:T(8,128)(2,1)}, bf16[448,1152]{1,0:T(8,128)(2,1)S(1)}, u32[]{:S(2)}, u32[]{:S(2)}) collective-permute-start(bf16[448,1152]{1,0:T(8,128)(2,1)} %pad_maximum_fusion), channel_id=1, source_target_pairs={{0,8},{8,0},{16,24},{24,16},{32,40},{40,32},{48,56},{56,48},{64,72... | collective-permute-start | bytes 3096584 | tf_op jit(solution)/shard_map/ppermute | solution.py:22
  27.4 2.5 %collective-permute-start.15 = (bf16[16,56]{1,0:T(8,128)(2,1)S(1)}, bf16[16,56]{1,0:T(8,128)(2,1)S(1)}, u32[]{:S(2)}, u32[]{:S(2)}) collective-permute-start(bf16[16,56]{1,0:T(8,128)(2,1)S(1)} %slice.245), channel_id=1, source_target_pairs={{0,1},{1,0},{2,3},{3,2},{4,5},{5,4},{6,7},{7,6},{8,9},{9,8},{10,11... | collective-permute-start | bytes 5384 | tf_op jit(solution)/shard_map/ppermute | solution.py:89
  30.0 4.0 %collective-permute-start.16 = (bf16[16,112]{1,0:T(8,128)(2,1)S(1)}, bf16[16,112]{1,0:T(8,128)(2,1)S(1)}, u32[]{:S(2)}, u32[]{:S(2)}) collective-permute-start(bf16[16,112]{1,0:T(8,128)(2,1)S(1)} %reshape.31), channel_id=1, source_target_pairs={{0,2},{1,3},{2,0},{3,1},{4,6},{5,7},{6,4},{7,5},{8,10},{9,11},{10,... | collective-permute-start | bytes 10760 | tf_op jit(solution)/shard_map/ppermute | solution.py:89
  34.1 7.8 %collective-permute-start.17 = (bf16[16,224]{1,0:T(8,128)(2,1)S(1)}, bf16[16,224]{1,0:T(8,128)(2,1)S(1)}, u32[]{:S(2)}, u32[]{:S(2)}) collective-permute-start(bf16[16,224]{1,0:T(8,128)(2,1)S(1)} %reshape.32), channel_id=1, source_target_pairs={{0,4},{1,5},{2,6},{3,7},{4,0},{5,1},{6,2},{7,3},{8,12},{9,13},{10,... | collective-permute-start | bytes 21512 | tf_op jit(solution)/shard_map/ppermute | solution.py:89
  40.9 29.1 %collective-permute-start.5 = (bf16[448,1152]{1,0:T(8,128)(2,1)S(1)}, bf16[448,1152]{1,0:T(8,128)(2,1)S(1)}, u32[]{:S(2)}, u32[]{:S(2)}) collective-permute-start(bf16[448,1152]{1,0:T(8,128)(2,1)S(1)} %collective-permute-done.1), channel_id=1, source_target_pairs={{0,16},{8,120},{16,32},{24,8},{32,48},{40,24},{48,64},{56,40},{64,... | collective-permute-start | bytes 3096584 | tf_op jit(solution)/shard_map/ppermute | solution.py:31
  41.8 24.0 %collective-permute-start.3 = (bf16[448,1152]{1,0:T(8,128)(2,1)S(1)}, bf16[448,1152]{1,0:T(8,128)(2,1)}, u32[]{:S(2)}, u32[]{:S(2)}) collective-permute-start(bf16[448,1152]{1,0:T(8,128)(2,1)S(1)} %collective-permute-done), channel_id=1, source_target_pairs={{0,16},{8,120},{16,32},{24,8},{32,48},{40,24},{48,64},{56,40},{64,... | collective-permute-start | bytes 3096584 | tf_op jit(solution)/shard_map/ppermute | solution.py:31
  41.9 31.7 %collective-permute-start.2 = (bf16[448,1152]{1,0:T(8,128)(2,1)S(1)}, bf16[448,1152]{1,0:T(8,128)(2,1)}, u32[]{:S(2)}, u32[]{:S(2)}) collective-permute-start(bf16[448,1152]{1,0:T(8,128)(2,1)S(1)} %collective-permute-done.1), channel_id=1, source_target_pairs={{0,8},{8,0},{16,24},{24,16},{32,40},{40,32},{48,56},{56,48},{64,72... | collective-permute-start | bytes 3096584 | tf_op jit(solution)/shard_map/ppermute | solution.py:22
  65.8 31.2 %collective-permute-start.7 = (bf16[448,1152]{1,0:T(8,128)(2,1)}, bf16[448,1152]{1,0:T(8,128)(2,1)S(1)}, u32[]{:S(2)}, u32[]{:S(2)}) collective-permute-start(bf16[448,1152]{1,0:T(8,128)(2,1)} %collective-permute-done.3), channel_id=1, source_target_pairs={{0,16},{8,120},{16,32},{24,8},{32,48},{40,24},{48,64},{56,40},{64,... | collective-permute-start | bytes 3096584 | tf_op jit(solution)/shard_map/ppermute | solution.py:31
  67.7 32.3 %collective-permute-start.4 = (bf16[448,1152]{1,0:T(8,128)(2,1)}, bf16[448,1152]{1,0:T(8,128)(2,1)S(1)}, u32[]{:S(2)}, u32[]{:S(2)}) collective-permute-start(bf16[448,1152]{1,0:T(8,128)(2,1)} %collective-permute-done.3), channel_id=1, source_target_pairs={{0,8},{8,0},{16,24},{24,16},{32,40},{40,32},{48,56},{56,48},{64,72... | collective-permute-start | bytes 3096584 | tf_op jit(solution)/shard_map/ppermute | solution.py:22
  69.9 20.9 %collective-permute-start.9 = (bf16[448,1152]{1,0:T(8,128)(2,1)S(1)}, bf16[448,1152]{1,0:T(8,128)(2,1)S(1)}, u32[]{:S(2)}, u32[]{:S(2)}) collective-permute-start(bf16[448,1152]{1,0:T(8,128)(2,1)S(1)} %collective-permute-done.5), channel_id=1, source_target_pairs={{0,16},{8,120},{16,32},{24,8},{32,48},{40,24},{48,64},{56,40},{64,... | collective-permute-start | bytes 3096584 | tf_op jit(solution)/shard_map/ppermute | solution.py:31
  73.6 28.8 %collective-permute-start.6 = (bf16[448,1152]{1,0:T(8,128)(2,1)S(1)}, bf16[448,1152]{1,0:T(8,128)(2,1)S(1)}, u32[]{:S(2)}, u32[]{:S(2)}) collective-permute-start(bf16[448,1152]{1,0:T(8,128)(2,1)S(1)} %collective-permute-done.5), channel_id=1, source_target_pairs={{0,8},{8,0},{16,24},{24,16},{32,40},{40,32},{48,56},{56,48},{64,72... | collective-permute-start | bytes 3096584 | tf_op jit(solution)/shard_map/ppermute | solution.py:22
  90.8 15.8 %collective-permute-start.13 = (bf16[448,1152]{1,0:T(8,128)(2,1)S(1)}, bf16[448,1152]{1,0:T(8,128)(2,1)S(1)}, u32[]{:S(2)}, u32[]{:S(2)}) collective-permute-start(bf16[448,1152]{1,0:T(8,128)(2,1)S(1)} %collective-permute-done.9), channel_id=1, source_target_pairs={{0,16},{8,120},{16,32},{24,8},{32,48},{40,24},{48,64},{56,40},{64,... | collective-permute-start | bytes 3096584 | tf_op jit(solution)/shard_map/ppermute | solution.py:31
  93.6 32.6 %collective-permute-start.10 = (bf16[448,1152]{1,0:T(8,128)(2,1)S(1)}, bf16[448,1152]{1,0:T(8,128)(2,1)S(1)}, u32[]{:S(2)}, u32[]{:S(2)}) collective-permute-start(bf16[448,1152]{1,0:T(8,128)(2,1)S(1)} %collective-permute-done.9), channel_id=1, source_target_pairs={{0,8},{8,0},{16,24},{24,16},{32,40},{40,32},{48,56},{56,48},{64,72... | collective-permute-start | bytes 3096584 | tf_op jit(solution)/shard_map/ppermute | solution.py:22
  97.0 19.2 %collective-permute-start.11 = (bf16[448,1152]{1,0:T(8,128)(2,1)S(1)}, bf16[448,1152]{1,0:T(8,128)(2,1)S(1)}, u32[]{:S(2)}, u32[]{:S(2)}) collective-permute-start(bf16[448,1152]{1,0:T(8,128)(2,1)S(1)} %collective-permute-done.7), channel_id=1, source_target_pairs={{0,16},{8,120},{16,32},{24,8},{32,48},{40,24},{48,64},{56,40},{64,... | collective-permute-start | bytes 3096584 | tf_op jit(solution)/shard_map/ppermute | solution.py:31
  100.0 23.9 %collective-permute-start.8 = (bf16[448,1152]{1,0:T(8,128)(2,1)S(1)}, bf16[448,1152]{1,0:T(8,128)(2,1)S(1)}, u32[]{:S(2)}, u32[]{:S(2)}) collective-permute-start(bf16[448,1152]{1,0:T(8,128)(2,1)S(1)} %collective-permute-done.7), channel_id=1, source_target_pairs={{0,8},{8,0},{16,24},{24,16},{32,40},{40,32},{48,56},{56,48},{64,72... | collective-permute-start | bytes 3096584 | tf_op jit(solution)/shard_map/ppermute | solution.py:22
  106.6 27.2 %collective-permute-start.14 = (bf16[448,1152]{1,0:T(8,128)(2,1)S(1)}, bf16[448,1152]{1,0:T(8,128)(2,1)S(1)}, u32[]{:S(2)}, u32[]{:S(2)}) collective-permute-start(bf16[448,1152]{1,0:T(8,128)(2,1)S(1)} %collective-permute-done.13), channel_id=1, source_target_pairs={{0,8},{8,0},{16,24},{24,16},{32,40},{40,32},{48,56},{56,48},{64,72... | collective-permute-start | bytes 3096584 | tf_op jit(solution)/shard_map/ppermute | solution.py:22
  116.3 14.2 %collective-permute-start.12 = (bf16[448,1152]{1,0:T(8,128)(2,1)S(1)}, bf16[448,1152]{1,0:T(8,128)(2,1)S(1)}, u32[]{:S(2)}, u32[]{:S(2)}) collective-permute-start(bf16[448,1152]{1,0:T(8,128)(2,1)S(1)} %collective-permute-done.11), channel_id=1, source_target_pairs={{0,8},{8,0},{16,24},{24,16},{32,40},{40,32},{48,56},{56,48},{64,72... | collective-permute-start | bytes 3096584 | tf_op jit(solution)/shard_map/ppermute | solution.py:22

commit v2 on v1

v2 whole, which is shorter than its diff:
```python
import jax
import jax.numpy as jnp
from jax import lax
from jax.experimental import pallas as pl
from jax.experimental.pallas import tpu as pltpu
from jax.sharding import PartitionSpec as P

SITE_ROWS = ("site", "rows")
SITE_ROWS_WIDTH = ("site", "rows", "width")
SITE_WIDTH = ("site", "width")
EARLY = (144, 112)
CUTS = (0, 144, 256, 448)
LAST = 128


def spread(row, lane, count):
    rows = lax.broadcasted_iota(jnp.int32, (count, row.shape[1]), 0) + lane
    lanes = lax.broadcasted_iota(jnp.int32, (count, row.shape[1]), 1)
    return jnp.sum(jnp.where(rows == lanes, jnp.broadcast_to(row, rows.shape), 0.0), axis=1, keepdims=True)


def mixed(share, pairs, norm, n):
    depth = share.shape[0]
    widths = [one.shape[1] for one, _ in pairs]
    total = sum(widths)
    arrays = [a for pair in pairs for a in pair]
    gains = [a.reshape(1, -1) for a in norm]
    wide = total + gains[0].shape[1]
    cuts = list(zip(CUTS, CUTS[1:]))
    starts = [0, EARLY[0], sum(EARLY), depth]

    def kernel(*refs):
        share_ref, refs = refs[0], refs[1:]
        array_refs, refs = refs[: len(arrays)], refs[len(arrays) :]
        train_ref, step_ref, *whole_refs, top_ref = refs[:6]
        refs = refs[6:]
        share_buf, array_bufs, gain_bufs = refs[0], refs[1 : 1 + len(arrays)], refs[1 + len(arrays) : 3 + len(arrays)]
        sems, small_sems = refs[-2:]
        small = [
            pltpu.make_async_copy(src, dst, small_sems.at[k])
            for k, (src, dst) in enumerate(
                ((share_ref, share_buf), (train_ref, gain_bufs[0]), (step_ref, gain_bufs[1]))
            )
        ]
        for copy in small:
            copy.start()
        large = []
        for c, (low, high) in enumerate(cuts):
            large.append(
                [
                    pltpu.make_async_copy(src.at[low:high], dst.at[low:high], sems.at[c, k])
                    for k, (src, dst) in enumerate(zip(array_refs, array_bufs))
                ]
            )
            for copy in large[-1]:
                copy.start()
        for copy in small:
            copy.wait()
        gain = (gain_bufs[0][...] + gain_bufs[1][...]).astype(jnp.bfloat16).astype(jnp.float32)
        top_ref[:, :, total:] = jnp.broadcast_to(gain[None], (n, 1, wide - total))
        tops = [None] * len(widths)
        for c, (low, high) in enumerate(cuts):
            column = spread(share_buf[...], low, high - low)
            rest = 1.0 - column
            for copy in large[c]:
                copy.wait()
            at = 0
            for k, w in enumerate(widths):
                whole = column * array_bufs[2 * k][low:high, :] + rest * array_bufs[2 * k + 1][low:high, :]
                piece = max(p for p in range(3) if starts[p] <= low)
                whole_refs[piece][low - starts[piece] : high - starts[piece], at : at + w] = whole
                top = jnp.max(jnp.abs(whole), axis=0, keepdims=True)
                tops[k] = top if c == 0 else jnp.maximum(tops[k], top)
                at += w
        at = 0
        for top, w in zip(tops, widths):
            top_ref[:, :, at : at + w] = jnp.broadcast_to(top[None], (n, 1, w))
            at += w

    inputs = [share.reshape(1, depth), *arrays, *gains]
    return pl.pallas_call(
        kernel,
        in_specs=[pl.BlockSpec(memory_space=pltpu.HBM)] * len(inputs),
        out_specs=[pl.BlockSpec(memory_space=pltpu.VMEM)] * 4,
        out_shape=[jax.ShapeDtypeStruct((b - a, total), jnp.float32) for a, b in zip(starts, starts[1:])]
        + [jax.ShapeDtypeStruct((n, 1, wide), jnp.float32)],
        scratch_shapes=[pltpu.VMEM((1, depth), jnp.float32)]
        + [pltpu.VMEM(a.shape, jnp.float32) for a in arrays]
        + [pltpu.VMEM(g.shape, jnp.float32) for g in gains]
        + [pltpu.SemaphoreType.DMA((len(cuts), len(arrays))), pltpu.SemaphoreType.DMA((3,))],
        compiler_params=pltpu.CompilerParams(vmem_limit_bytes=67043328),
        cost_estimate=pl.CostEstimate(flops=6 * depth * total, bytes_accessed=12 * depth * total, transcendentals=0),
    )(*inputs)


def place(outs, block, hops, flip, skip, depth, shapes):
    n = lax.axis_size("rows")
    ends = [0]
    for shape in shapes:
        ends.append(ends[-1] + shape[1])
    rows = block.shape[0]

    def kernel(*refs):
        block_ref, out_refs, sems = refs[0], refs[-1 - len(shapes) : -1], refs[-1]
        me = lax.axis_index("rows")
        core = me & 1
        owner = ((me - core - (2 - 4 * core) * hops) & (n - 1)) + (core ^ flip)
        at = pl.multiple_of(owner * depth + skip, 32)
        copies = [
            pltpu.make_async_copy(block_ref.at[:, b:e], out.at[pl.ds(at, rows), :], sems.at[k])
            for k, (out, b, e) in enumerate(zip(out_refs, ends, ends[1:]))
        ]
        for copy in copies:
            copy.start()
        for copy in copies:
            copy.wait()

    anywhere = [pl.BlockSpec(memory_space=pltpu.HBM)] * len(shapes)
    given = [] if outs is None else list(outs)
    return pl.pallas_call(
        kernel,
        in_specs=[pl.BlockSpec(memory_space=pltpu.VMEM)] + anywhere[: len(given)],
        out_specs=anywhere,
        out_shape=[jax.ShapeDtypeStruct(shape, jnp.bfloat16) for shape in shapes],
        input_output_aliases={1 + k: k for k in range(len(given))},
        scratch_shapes=[pltpu.SemaphoreType.DMA((len(shapes),))],
        compiler_params=pltpu.CompilerParams(vmem_limit_bytes=4 << 20),
        cost_estimate=pl.CostEstimate(flops=2 * block.size, bytes_accessed=4 * block.size, transcendentals=0),
    )(block, *given)


def partner(array):
    n = lax.axis_size("rows")
    return lax.ppermute(array, "rows", [(i, i ^ 1) for i in range(n)])


def onward(array):
    n = lax.axis_size("rows")

    def to(i):
        return (i + 2) % n if i % 2 == 0 else (i - 2) % n

    return lax.ppermute(array, "rows", [(i, to(i)) for i in range(n)])


def body(one_query, other_query, one_key, other_key, one_value, other_value, mix_share, norm_train, norm_step):
    n = lax.axis_size("rows")
    wide = lax.axis_size("width")
    depth = one_query.shape[0]
    pairs = [(one_query, other_query), (one_key, other_key), (one_value, other_value)]
    widths = [one.shape[1] for one, _ in pairs]
    ends = [0, widths[0], widths[0] + widths[1], sum(widths)]
    *early, late, tops = mixed(mix_share, pairs, (norm_train, norm_step), n)
    coming = [onward(early[0]), onward(early[1])]
    seen = lax.all_to_all(tops, "rows", split_axis=0, concat_axis=0, tiled=True)
    scale = seen.max(axis=(0, 1))
    scales = [scale[b:e] for b, e in zip(ends, ends[1:])]
    scale = scale[: ends[3]]
    norms = seen[:, 0, ends[3] :].astype(jnp.bfloat16)

    def scaled(whole):
        return lax.optimization_barrier((whole / scale).astype(jnp.bfloat16))

    mine_b = scaled(late)
    *early, mine_b, scale = lax.optimization_barrier((*early, mine_b, scale))
    mine = jnp.concatenate([(a / scale).astype(jnp.bfloat16) for a in early] + [mine_b], axis=0)
    shapes = [(n * depth, w) for w in widths]

    def put(outs, block, hops, flip, skip=0):
        return place(outs, block, hops, flip, skip, depth, shapes)

    outs = put(None, mine, 0, 0)
    sibling = partner(mine)
    *coming, scale_in, _ = lax.optimization_barrier((*coming, scale, sibling))
    come = [(a / scale_in).astype(jnp.bfloat16) for a in coming]
    outs = put(outs, sibling, 0, 1)
    units = [mine, sibling]
    steps = n // 2 - 1
    for step in range(1, steps + 1):
        hop, chain = (step + 1) // 2, (step + 1) % 2
        if step == steps:
            cuts = [(step, 0, depth - LAST), (step + 1, depth - LAST, depth)]
        else:
            cuts = [(step, 0, depth)]
        for k, low, high in cuts:
            if k == 1:
                here = onward(mine_b)
                here = jnp.concatenate([*come, here], axis=0)
            else:
                here = onward(units[step - 1][low:high])
            outs = put(outs, here, hop, chain, low)
            across = partner(here)
            outs = put(outs, across, -hop, 1 ^ chain, low)
        units.append(here)

    k, turn = 1, 1
    while k < wide:
        other = lax.ppermute(norms, "width", [(i, i ^ k) for i in range(wide)])
        low = (lax.axis_index("width") & k) == 0
        a, b = jnp.where(low, norms, other), jnp.where(low, other, norms)
        norms = jnp.concatenate([a[:, None], b[:, None]], axis=1).reshape(n, -1)
        k *= 2
        turn += 1
    norms = norms.reshape(-1)
    return (*outs, *scales, norms)


def solution(mesh):
    return jax.shard_map(
        body,
        mesh=mesh,
        in_specs=(P(SITE_ROWS, "width"),) * 6 + (P(SITE_ROWS), P(SITE_ROWS_WIDTH), P(SITE_ROWS_WIDTH)),
        out_specs=(P("site", "width"),) * 3 + (P(SITE_WIDTH),) * 3 + (P("site"),),
        check_vma=False,
    )
```

time: 136 us -> 153 us (1.12)
  Pallas kernels: 0.01 us -> 35.1 us
  local copies, waits for them, and re-layouts: 30.6 us -> 4.06 us
  starting transfers between devices: 49.8 us -> 29.9 us
  blocking collectives: 0 us -> 18.2 us
  waiting for transfers between devices: 46.9 us -> 61.9 us
  other arithmetic: 7.26 us -> 1.69 us
    pallas_call x1 -> x19, Pallas kernels: 0.01 us -> 35.1 us  [the longest x18 31.4 us: place(): pl.pallas_call(kernel, in_specs=[pl.BlockSpec(memory_space=pltpu.VMEM)] +...]
    dynamic_update_slice x30 -> x0, local copies, waits for them, and re-layouts: 28.9 us -> none  [put(): lax.dynamic_update_slice(out, block[:, b:e], (at, jnp.int32(0)), allow_ne...]
    ppermute x7 -> x10, waiting for transfers between devices: 36.3 us -> 59.6 us  [onward(): return lax.ppermute(array, 'rows', [(i, to(i)) for i in range(n)])]
    all_to_all x0 -> x1, blocking collectives: none -> 18.2 us  [body(): seen = lax.all_to_all(tops, 'rows', split_axis=0, concat_axis=0, tiled=True)]
    all_to_all x1 -> x0, starting transfers between devices: 9.97 us -> none  [body(): lax.all_to_all(jnp.broadcast_to(own, (n, own.shape[0])), 'rows', split_ax...]
    all_to_all x1 -> x0, waiting for transfers between devices: 8.1 us -> none  [body(): lax.all_to_all(jnp.broadcast_to(own, (n, own.shape[0])), 'rows', split_ax...]
    ppermute x8 -> x9, starting transfers between devices: 21.2 us -> 15.2 us  [partner(): return lax.ppermute(array, 'rows', [(i, i ^ 1) for i in range(n)])]
    ppermute x7 -> x10, starting transfers between devices: 11.7 us -> 7.64 us  [onward(): return lax.ppermute(array, 'rows', [(i, to(i)) for i in range(n)])]
  transfers between devices with their start and end apart: 19 -> 22, of which waited for: 7 -> 11; matrix products, arithmetic and copies ran while one was open for 21% -> 2% of each run, Pallas kernels for 0% -> 20%
where the time goes in v2:
time: 153 us; the launch traced here: 152 us
  waiting for transfers between devices  61.9 us (40%)
  Pallas kernels  35.1 us (23%)
  starting transfers between devices  29.9 us (20%)
  blocking collectives  18.2 us (12%)
  local copies, waits for them, and re-layouts  4.06 us (3%)
  other arithmetic  1.69 us (1%)
    ppermute x10, waiting for transfers between devices, onward(): return lax.ppermute(array, 'rows', [(i, to(i)) for i in range(n)])  59.6 us
    pallas_call x18, Pallas kernels, place(): pl.pallas_call(kernel, in_specs=[pl.BlockSpec(memory_space=pltpu.VMEM)] +...  31.4 us
    all_to_all x1, blocking collectives, body(): seen = lax.all_to_all(tops, 'rows', split_axis=0, concat_axis=0, tiled=True)  18.2 us
    ppermute x9, starting transfers between devices, partner(): return lax.ppermute(array, 'rows', [(i, i ^ 1) for i in range(n)])  15.2 us
    ppermute x10, starting transfers between devices, onward(): return lax.ppermute(array, 'rows', [(i, to(i)) for i in range(n)])  7.64 us
    ppermute x3, starting transfers between devices, body(): other = lax.ppermute(norms, 'width', [(i, i ^ k) for i in range(wide)])  6.97 us
    pallas_call x1, Pallas kernels, mixed(): pl.pallas_call(kernel, in_specs=[pl.BlockSpec(memory_space=pltpu.HBM)] *...  3.7 us
  transfers between devices with their start and end apart: 22, of which 11 were waited for; matrix products, arithmetic and copies ran while one was open for 2% of the time, Pallas kernels for 20%

profile of v2, /device:TPU:1, one launch (start us, length us, event | category | flops | bytes accessed | tf_op | source)
XLA Modules:
  0.0 151.9 jit_solution(15244460098948378337)
XLA Ops:
  0.6 3.7 %shard_map.144 = (f32[144,1152]{1,0:T(8,128)}, f32[112,1152]{1,0:T(8,128)}, f32[192,1152]{1,0:T(8,128)}, f32[16,1,1208]{2,1,0:T(1,128)}) custom-call(f32[1,448]{1,0:T(1,128)} %bitcast.27, f32[448,896]{1,0:T(8,128)} %refs_1_.1, f32[448,896]{1,0:T(8,128)} %refs_2_.1, f32[448,128]{1,0:T(8,128)} %refs_3_.1, f32[448,128]{1,0:T(8,128)} %refs_4_.1, ...), custom_call_target="tpu_custom_call" | custom-call | flops 3096576 | bytes 6193152 | tf_op jit(solution)/shard_map/pallas_call | solution.py:81
  4.4 18.2 %all_to_all.5 = f32[16,1,1208]{2,1,0:T(1,128)S(1)} all-to-all(f32[16,1,1208]{2,1,0:T(1,128)} %get-tuple-element.75), channel_id=1, replica_groups=mesh['site'=2,'rows'=16,'width'=8] {'rows'}, dimensions={0} | all-to-all | bytes 154624 | tf_op jit(solution)/shard_map/all_to_all | solution.py:155
  22.6 1.2 divide_convert_fusion
  25.8 13.8 %collective-permute-done.1 = f32[112,1152]{1,0:T(8,128)S(1)} collective-permute-done((f32[112,1152]{1,0:T(8,128)S(1)}, f32[112,1152]{1,0:T(8,128)S(1)}, u32[]{:S(2)}, u32[]{:S(2)}) %collective-permute-start.1) | collective-permute-done | bytes 516128 | tf_op jit(solution)/shard_map/ppermute | solution.py:143
  39.7 1.1 collective-permute-start.10
  40.8 3.6 %collective-permute-done.3 = bf16[192,1152]{1,0:T(8,128)(2,1)S(1)} collective-permute-done((bf16[192,1152]{1,0:T(8,128)(2,1)S(1)}, bf16[192,1152]{1,0:T(8,128)(2,1)S(1)}, u32[]{:S(2)}, u32[]{:S(2)}) %collective-permute-start.3) | collective-permute-done | bytes 442400 | tf_op jit(solution)/shard_map/ppermute | solution.py:143
  44.5 1.1 collective-permute-start.4
  45.5 10.0 %collective-permute-done.10.refs_0_ = bf16[448,1152]{1,0:T(8,128)(2,1)} collective-permute-done((bf16[448,1152]{1,0:T(8,128)(2,1)S(1)}, bf16[448,1152]{1,0:T(8,128)(2,1)}, u32[]{:S(2)}, u32[]{:S(2)}) %collective-permute-start.10) | collective-permute-done | bytes 1032224 | tf_op jit(solution)/shard_map/ppermute | solution.py:143
  55.5 1.0 collective-permute-start.11
  56.5 10.1 %collective-permute-done.4.refs_0_ = bf16[448,1152]{1,0:T(8,128)(2,1)} collective-permute-done((bf16[448,1152]{1,0:T(8,128)(2,1)S(1)}, bf16[448,1152]{1,0:T(8,128)(2,1)}, u32[]{:S(2)}, u32[]{:S(2)}) %collective-permute-start.4) | collective-permute-done | bytes 1032224 | tf_op jit(solution)/shard_map/ppermute | solution.py:143
  66.6 1.0 collective-permute-start.5
  67.6 1.3 collective-permute-start.19
  68.9 2.0 %collective-permute-start.18 = (bf16[448,1152]{1,0:T(8,128)(2,1)S(1)}, bf16[448,1152]{1,0:T(8,128)(2,1)}, u32[]{:S(2)}, u32[]{:S(2)}) collective-permute-start(bf16[448,1152]{1,0:T(8,128)(2,1)S(1)} %pad_maximum_fusion.1.refs_0_), channel_id=1, source_target_pairs={{0,8},{8,0},{16,24},{24,16},{32,40},{40,32},{48,56},{56,48},{64,72... | collective-permute-start | bytes 3096584 | tf_op jit(solution)/shard_map/ppermute | solution.py:134
  70.9 6.8 %collective-permute-done.11.refs_0_ = bf16[448,1152]{1,0:T(8,128)(2,1)} collective-permute-done((bf16[448,1152]{1,0:T(8,128)(2,1)}, bf16[448,1152]{1,0:T(8,128)(2,1)}, u32[]{:S(2)}, u32[]{:S(2)}) %collective-permute-start.11) | collective-permute-done | bytes 1032224 | tf_op jit(solution)/shard_map/ppermute | solution.py:143
  77.7 1.0 collective-permute-start.12
  78.8 2.8 %collective-permute-start.20 = (bf16[16,112]{1,0:T(8,128)(2,1)S(1)}, bf16[16,112]{1,0:T(8,128)(2,1)S(1)}, u32[]{:S(2)}, u32[]{:S(2)}) collective-permute-start(bf16[16,112]{1,0:T(8,128)(2,1)S(1)} %reshape.36), channel_id=1, source_target_pairs={{0,2},{1,3},{2,0},{3,1},{4,6},{5,7},{6,4},{7,5},{8,10},{9,11},{10,... | collective-permute-start | bytes 10760 | tf_op jit(solution)/shard_map/ppermute | solution.py:198
  81.5 1.2 collective-permute-done.20
  82.7 2.8 %collective-permute-start.16 = (bf16[448,1152]{1,0:T(8,128)(2,1)}, bf16[448,1152]{1,0:T(8,128)(2,1)}, u32[]{:S(2)}, u32[]{:S(2)}) collective-permute-start(bf16[448,1152]{1,0:T(8,128)(2,1)} %collective-permute-done.4.refs_0_), channel_id=1, source_target_pairs={{0,8},{8,0},{16,24},{24,16},{32,40},{40,32},{48,56},{56,48},{64,72... | collective-permute-start | bytes 3096584 | tf_op jit(solution)/shard_map/ppermute | solution.py:134
  85.7 2.9 %collective-permute-done.5.refs_0_ = bf16[448,1152]{1,0:T(8,128)(2,1)S(1)} collective-permute-done((bf16[448,1152]{1,0:T(8,128)(2,1)}, bf16[448,1152]{1,0:T(8,128)(2,1)S(1)}, u32[]{:S(2)}, u32[]{:S(2)}) %collective-permute-start.5) | collective-permute-done | bytes 1032224 | tf_op jit(solution)/shard_map/ppermute | solution.py:143
  88.6 2.9 %collective-permute-start.21 = (bf16[16,224]{1,0:T(8,128)(2,1)S(1)}, bf16[16,224]{1,0:T(8,128)(2,1)S(1)}, u32[]{:S(2)}, u32[]{:S(2)}) collective-permute-start(bf16[16,224]{1,0:T(8,128)(2,1)S(1)} %reshape.37), channel_id=1, source_target_pairs={{0,4},{1,5},{2,6},{3,7},{4,0},{5,1},{6,2},{7,3},{8,12},{9,13},{10,... | collective-permute-start | bytes 21512 | tf_op jit(solution)/shard_map/ppermute | solution.py:198
  91.6 1.0 collective-permute-done.21
  92.6 1.0 collective-permute-start.8
  93.6 2.8 %collective-permute-start.15 = (bf16[448,1152]{1,0:T(8,128)(2,1)}, bf16[448,1152]{1,0:T(8,128)(2,1)}, u32[]{:S(2)}, u32[]{:S(2)}) collective-permute-start(bf16[448,1152]{1,0:T(8,128)(2,1)} %collective-permute-done.11.refs_0_), channel_id=1, source_target_pairs={{0,8},{8,0},{16,24},{24,16},{32,40},{40,32},{48,56},{56,48},{64,72... | collective-permute-start | bytes 3096584 | tf_op jit(solution)/shard_map/ppermute | solution.py:134
  96.5 3.2 %collective-permute-done.12.refs_0_ = bf16[448,1152]{1,0:T(8,128)(2,1)} collective-permute-done((bf16[448,1152]{1,0:T(8,128)(2,1)}, bf16[448,1152]{1,0:T(8,128)(2,1)}, u32[]{:S(2)}, u32[]{:S(2)}) %collective-permute-start.12) | collective-permute-done | bytes 1032224 | tf_op jit(solution)/shard_map/ppermute | solution.py:143
  99.8 2.7 %collective-permute-start.13 = (bf16[448,1152]{1,0:T(8,128)(2,1)}, bf16[448,1152]{1,0:T(8,128)(2,1)}, u32[]{:S(2)}, u32[]{:S(2)}) collective-permute-start(bf16[448,1152]{1,0:T(8,128)(2,1)} %collective-permute-done.12.refs_0_), channel_id=1, source_target_pairs={{0,8},{8,0},{16,24},{24,16},{32,40},{40,32},{48,56},{56,48},{64,72... | collective-permute-start | bytes 3096584 | tf_op jit(solution)/shard_map/ppermute | solution.py:134
  102.4 5.2 %collective-permute-done.8.refs_0_ = bf16[320,1152]{1,0:T(8,128)(2,1)} collective-permute-done((bf16[320,1152]{1,0:T(8,128)(2,1)S(1)}, bf16[320,1152]{1,0:T(8,128)(2,1)}, u32[]{:S(2)}, u32[]{:S(2)}) %collective-permute-start.8) | collective-permute-done | bytes 737312 | tf_op jit(solution)/shard_map/ppermute | solution.py:143
  107.7 2.7 %collective-permute-start.9 = (bf16[320,1152]{1,0:T(8,128)(2,1)}, bf16[320,1152]{1,0:T(8,128)(2,1)}, u32[]{:S(2)}, u32[]{:S(2)}) collective-permute-start(bf16[320,1152]{1,0:T(8,128)(2,1)} %collective-permute-done.8.refs_0_), channel_id=1, source_target_pairs={{0,8},{8,0},{16,24},{24,16},{32,40},{40,32},{48,56},{56,48},{64,72... | collective-permute-start | bytes 2211848 | tf_op jit(solution)/shard_map/ppermute | solution.py:134
  111.7 1.0 shard_map.145
  113.2 4.0 %collective-permute-done.6.refs_0_ = bf16[128,1152]{1,0:T(8,128)(2,1)S(1)} collective-permute-done((bf16[128,1152]{1,0:T(8,128)(2,1)}, bf16[128,1152]{1,0:T(8,128)(2,1)S(1)}, u32[]{:S(2)}, u32[]{:S(2)}) %collective-permute-start.6) | collective-permute-done | bytes 294944 | tf_op jit(solution)/shard_map/ppermute | solution.py:143
  117.1 2.1 %collective-permute-start.7 = (bf16[128,1152]{1,0:T(8,128)(2,1)S(1)}, bf16[128,1152]{1,0:T(8,128)(2,1)S(1)}, u32[]{:S(2)}, u32[]{:S(2)}) collective-permute-start(bf16[128,1152]{1,0:T(8,128)(2,1)S(1)} %collective-permute-done.6.refs_0_), channel_id=1, source_target_pairs={{0,8},{8,0},{16,24},{24,16},{32,40},{40,32},{48,56},{56,48},{64,72... | collective-permute-start | bytes 884744 | tf_op jit(solution)/shard_map/ppermute | solution.py:134
  120.0 1.2 copy-done.1
  121.2 1.0 shard_map.146
  122.2 1.0 shard_map.147
  123.2 2.2 %shard_map.148 = (bf16[7168,896]{1,0:T(8,128)(2,1)}, bf16[7168,128]{1,0:T(8,128)(2,1)}, bf16[7168,128]{1,0:T(8,128)(2,1)}) custom-call(bf16[448,1152]{1,0:T(8,128)(2,1)} %collective-permute-done.18.refs_0_, bf16[7168,896]{1,0:T(8,128)(2,1)} %get-tuple-element.89.refs_1_, ...), custom_call_target="tpu_custom_call", output_to_operand_aliasing={{0}: (1, {}), {1}: (2, {}), {2}: (3, {})} | custom-call | flops 1032192 | bytes 2064384 | tf_op jit(solution)/shard_map/pallas_call | solution.py:120
  125.4 2.2 %shard_map.149 = (bf16[7168,896]{1,0:T(8,128)(2,1)}, bf16[7168,128]{1,0:T(8,128)(2,1)}, bf16[7168,128]{1,0:T(8,128)(2,1)}) custom-call(bf16[448,1152]{1,0:T(8,128)(2,1)} %collective-permute-done.10.refs_0_, bf16[7168,896]{1,0:T(8,128)(2,1)} %get-tuple-element.92.refs_1_, ...), custom_call_target="tpu_custom_call", output_to_operand_aliasing={{0}: (1, {}), {1}: (2, {}), {2}: (3, {})} | custom-call | flops 1032192 | bytes 2064384 | tf_op jit(solution)/shard_map/pallas_call | solution.py:120
  127.6 2.2 %shard_map.150 = (bf16[7168,896]{1,0:T(8,128)(2,1)}, bf16[7168,128]{1,0:T(8,128)(2,1)}, bf16[7168,128]{1,0:T(8,128)(2,1)}) custom-call(bf16[448,1152]{1,0:T(8,128)(2,1)} %collective-permute-done.17.refs_0_, bf16[7168,896]{1,0:T(8,128)(2,1)} %get-tuple-element.95.refs_1_, ...), custom_call_target="tpu_custom_call", output_to_operand_aliasing={{0}: (1, {}), {1}: (2, {}), {2}: (3, {})} | custom-call | flops 1032192 | bytes 2064384 | tf_op jit(solution)/shard_map/pallas_call | solution.py:120
  129.8 2.2 %shard_map.151 = (bf16[7168,896]{1,0:T(8,128)(2,1)}, bf16[7168,128]{1,0:T(8,128)(2,1)}, bf16[7168,128]{1,0:T(8,128)(2,1)}) custom-call(bf16[448,1152]{1,0:T(8,128)(2,1)} %collective-permute-done.4.refs_0_, bf16[7168,896]{1,0:T(8,128)(2,1)} %get-tuple-element.98.refs_1_, ...), custom_call_target="tpu_custom_call", output_to_operand_aliasing={{0}: (1, {}), {1}: (2, {}), {2}: (3, {})} | custom-call | flops 1032192 | bytes 2064384 | tf_op jit(solution)/shard_map/pallas_call | solution.py:120
  132.0 2.2 %shard_map.152 = (bf16[7168,896]{1,0:T(8,128)(2,1)}, bf16[7168,128]{1,0:T(8,128)(2,1)}, bf16[7168,128]{1,0:T(8,128)(2,1)}) custom-call(bf16[448,1152]{1,0:T(8,128)(2,1)} %collective-permute-done.16.refs_0_, bf16[7168,896]{1,0:T(8,128)(2,1)} %get-tuple-element.101.refs_1_, ...), custom_call_target="tpu_custom_call", output_to_operand_aliasing={{0}: (1, {}), {1}: (2, {}), {2}: (3, {})} | custom-call | flops 1032192 | bytes 2064384 | tf_op jit(solution)/shard_map/pallas_call | solution.py:120
  134.2 2.2 %shard_map.153 = (bf16[7168,896]{1,0:T(8,128)(2,1)}, bf16[7168,128]{1,0:T(8,128)(2,1)}, bf16[7168,128]{1,0:T(8,128)(2,1)}) custom-call(bf16[448,1152]{1,0:T(8,128)(2,1)} %collective-permute-done.11.refs_0_, bf16[7168,896]{1,0:T(8,128)(2,1)} %get-tuple-element.104.refs_1_, ...), custom_call_target="tpu_custom_call", output_to_operand_aliasing={{0}: (1, {}), {1}: (2, {}), {2}: (3, {})} | custom-call | flops 1032192 | bytes 2064384 | tf_op jit(solution)/shard_map/pallas_call | solution.py:120
  136.4 2.2 %shard_map.154 = (bf16[7168,896]{1,0:T(8,128)(2,1)}, bf16[7168,128]{1,0:T(8,128)(2,1)}, bf16[7168,128]{1,0:T(8,128)(2,1)}) custom-call(bf16[448,1152]{1,0:T(8,128)(2,1)} %collective-permute-done.15.refs_0_, bf16[7168,896]{1,0:T(8,128)(2,1)} %get-tuple-element.107.refs_1_, ...), custom_call_target="tpu_custom_call", output_to_operand_aliasing={{0}: (1, {}), {1}: (2, {}), {2}: (3, {})} | custom-call | flops 1032192 | bytes 2064384 | tf_op jit(solution)/shard_map/pallas_call | solution.py:120
  138.6 1.0 shard_map.155
  139.6 2.2 %shard_map.156 = (bf16[7168,896]{1,0:T(8,128)(2,1)}, bf16[7168,128]{1,0:T(8,128)(2,1)}, bf16[7168,128]{1,0:T(8,128)(2,1)}) custom-call(bf16[448,1152]{1,0:T(8,128)(2,1)} %collective-permute-done.14.refs_0_, bf16[7168,896]{1,0:T(8,128)(2,1)} %get-tuple-element.113.refs_1_, ...), custom_call_target="tpu_custom_call", output_to_operand_aliasing={{0}: (1, {}), {1}: (2, {}), {2}: (3, {})} | custom-call | flops 1032192 | bytes 2064384 | tf_op jit(solution)/shard_map/pallas_call | solution.py:120
  141.8 2.2 %shard_map.157 = (bf16[7168,896]{1,0:T(8,128)(2,1)}, bf16[7168,128]{1,0:T(8,128)(2,1)}, bf16[7168,128]{1,0:T(8,128)(2,1)}) custom-call(bf16[448,1152]{1,0:T(8,128)(2,1)} %collective-permute-done.12.refs_0_, bf16[7168,896]{1,0:T(8,128)(2,1)} %get-tuple-element.116.refs_1_, ...), custom_call_target="tpu_custom_call", output_to_operand_aliasing={{0}: (1, {}), {1}: (2, {}), {2}: (3, {})} | custom-call | flops 1032192 | bytes 2064384 | tf_op jit(solution)/shard_map/pallas_call | solution.py:120
  144.0 2.2 %shard_map.158 = (bf16[7168,896]{1,0:T(8,128)(2,1)}, bf16[7168,128]{1,0:T(8,128)(2,1)}, bf16[7168,128]{1,0:T(8,128)(2,1)}) custom-call(bf16[448,1152]{1,0:T(8,128)(2,1)} %collective-permute-done.13.refs_0_, bf16[7168,896]{1,0:T(8,128)(2,1)} %get-tuple-element.119.refs_1_, ...), custom_call_target="tpu_custom_call", output_to_operand_aliasing={{0}: (1, {}), {1}: (2, {}), {2}: (3, {})} | custom-call | flops 1032192 | bytes 2064384 | tf_op jit(solution)/shard_map/pallas_call | solution.py:120
  146.2 2.0 %shard_map.159 = (bf16[7168,896]{1,0:T(8,128)(2,1)}, bf16[7168,128]{1,0:T(8,128)(2,1)}, bf16[7168,128]{1,0:T(8,128)(2,1)}) custom-call(bf16[320,1152]{1,0:T(8,128)(2,1)} %collective-permute-done.8.refs_0_, bf16[7168,896]{1,0:T(8,128)(2,1)} %get-tuple-element.122.refs_1_, ...), custom_call_target="tpu_custom_call", output_to_operand_aliasing={{0}: (1, {}), {1}: (2, {}), {2}: (3, {})} | custom-call | flops 737280 | bytes 1474560 | tf_op jit(solution)/shard_map/pallas_call | solution.py:120
  148.2 2.0 %shard_map.160 = (bf16[7168,896]{1,0:T(8,128)(2,1)}, bf16[7168,128]{1,0:T(8,128)(2,1)}, bf16[7168,128]{1,0:T(8,128)(2,1)}) custom-call(bf16[320,1152]{1,0:T(8,128)(2,1)} %collective-permute-done.9.refs_0_, bf16[7168,896]{1,0:T(8,128)(2,1)} %get-tuple-element.125.refs_1_, ...), custom_call_target="tpu_custom_call", output_to_operand_aliasing={{0}: (1, {}), {1}: (2, {}), {2}: (3, {})} | custom-call | flops 737280 | bytes 1474560 | tf_op jit(solution)/shard_map/pallas_call | solution.py:120
  150.2 0.7 shard_map.161
  151.0 0.7 shard_map.162
  (50 shorter events, 5.1 us)
Async XLA Ops:
  4.3 19.5 %copy-start.2 = (f32[144,1152]{1,0:T(8,128)S(1)}, f32[144,1152]{1,0:T(8,128)}, u32[]{:S(2)}) copy-start(f32[144,1152]{1,0:T(8,128)} %get-tuple-element.77) | copy-start | bytes 1990660
  4.4 19.6 %copy-start.3 = (f32[112,1152]{1,0:T(8,128)S(1)}, f32[112,1152]{1,0:T(8,128)}, u32[]{:S(2)}) copy-start(f32[112,1152]{1,0:T(8,128)} %get-tuple-element.78) | copy-start | bytes 1548292
  24.1 15.5 %collective-permute-start.2 = (bf16[448,1152]{1,0:T(8,128)(2,1)S(1)}, bf16[448,1152]{1,0:T(8,128)(2,1)S(1)}, u32[]{:S(2)}, u32[]{:S(2)}) collective-permute-start(bf16[448,1152]{1,0:T(8,128)(2,1)S(1)} %pad_maximum_fusion.refs_0_), channel_id=1, source_target_pairs={{0,8},{8,0},{16,24},{24,16},{32,40},{40,32},{48,56},{56,48},{64,72... | collective-permute-start | bytes 3096584 | tf_op jit(solution)/shard_map/ppermute | solution.py:134
  24.2 15.4 %collective-permute-start = (f32[144,1152]{1,0:T(8,128)S(1)}, f32[144,1152]{1,0:T(8,128)S(1)}, u32[]{:S(2)}, u32[]{:S(2)}) collective-permute-start(f32[144,1152]{1,0:T(8,128)S(1)} %copy-done.2), channel_id=1, source_target_pairs={{0,16},{8,120},{16,32},{24,8},{32,48},{40,24},{48,64},{56,40},{64,... | collective-permute-start | bytes 1990664 | tf_op jit(solution)/shard_map/ppermute | solution.py:143
  24.3 15.3 %collective-permute-start.1 = (f32[112,1152]{1,0:T(8,128)S(1)}, f32[112,1152]{1,0:T(8,128)S(1)}, u32[]{:S(2)}, u32[]{:S(2)}) collective-permute-start(f32[112,1152]{1,0:T(8,128)S(1)} %copy-done.3), channel_id=1, source_target_pairs={{0,16},{8,120},{16,32},{24,8},{32,48},{40,24},{48,64},{56,40},{64,... | collective-permute-start | bytes 1548296 | tf_op jit(solution)/shard_map/ppermute | solution.py:143
  25.1 19.3 %collective-permute-start.3 = (bf16[192,1152]{1,0:T(8,128)(2,1)S(1)}, bf16[192,1152]{1,0:T(8,128)(2,1)S(1)}, u32[]{:S(2)}, u32[]{:S(2)}) collective-permute-start(bf16[192,1152]{1,0:T(8,128)(2,1)S(1)} %divide_convert_fusion), channel_id=1, source_target_pairs={{0,16},{8,120},{16,32},{24,8},{32,48},{40,24},{48,64},{56,40},{64,... | collective-permute-start | bytes 1327112 | tf_op jit(solution)/shard_map/ppermute | solution.py:143
  39.6 4.8 %copy-start = (bf16[448,1152]{1,0:T(8,128)(2,1)}, bf16[448,1152]{1,0:T(8,128)(2,1)S(1)}, u32[]{:S(2)}) copy-start(bf16[448,1152]{1,0:T(8,128)(2,1)S(1)} %collective-permute-done.2.refs_0_) | copy-start | bytes 3096580
  39.7 15.8 %collective-permute-start.10 = (bf16[448,1152]{1,0:T(8,128)(2,1)S(1)}, bf16[448,1152]{1,0:T(8,128)(2,1)}, u32[]{:S(2)}, u32[]{:S(2)}) collective-permute-start(bf16[448,1152]{1,0:T(8,128)(2,1)S(1)} %collective-permute-done.2.refs_0_), channel_id=1, source_target_pairs={{0,16},{8,120},{16,32},{24,8},{32,48},{40,24},{48,64},{56,40},{64,... | collective-permute-start | bytes 3096584 | tf_op jit(solution)/shard_map/ppermute | solution.py:143
  44.5 22.1 %collective-permute-start.4 = (bf16[448,1152]{1,0:T(8,128)(2,1)S(1)}, bf16[448,1152]{1,0:T(8,128)(2,1)}, u32[]{:S(2)}, u32[]{:S(2)}) collective-permute-start(bf16[448,1152]{1,0:T(8,128)(2,1)S(1)} %pad_maximum_fusion.1.refs_0_), channel_id=1, source_target_pairs={{0,16},{8,120},{16,32},{24,8},{32,48},{40,24},{48,64},{56,40},{64,... | collective-permute-start | bytes 3096584 | tf_op jit(solution)/shard_map/ppermute | solution.py:143
  55.5 22.1 %collective-permute-start.11 = (bf16[448,1152]{1,0:T(8,128)(2,1)}, bf16[448,1152]{1,0:T(8,128)(2,1)}, u32[]{:S(2)}, u32[]{:S(2)}) collective-permute-start(bf16[448,1152]{1,0:T(8,128)(2,1)} %collective-permute-done.10.refs_0_), channel_id=1, source_target_pairs={{0,16},{8,120},{16,32},{24,8},{32,48},{40,24},{48,64},{56,40},{64,... | collective-permute-start | bytes 3096584 | tf_op jit(solution)/shard_map/ppermute | solution.py:143
  66.6 22.0 %collective-permute-start.5 = (bf16[448,1152]{1,0:T(8,128)(2,1)}, bf16[448,1152]{1,0:T(8,128)(2,1)S(1)}, u32[]{:S(2)}, u32[]{:S(2)}) collective-permute-start(bf16[448,1152]{1,0:T(8,128)(2,1)} %collective-permute-done.4.refs_0_), channel_id=1, source_target_pairs={{0,16},{8,120},{16,32},{24,8},{32,48},{40,24},{48,64},{56,40},{64,... | collective-permute-start | bytes 3096584 | tf_op jit(solution)/shard_map/ppermute | solution.py:143
  67.6 11.0 %collective-permute-start.19 = (bf16[16,56]{1,0:T(8,128)(2,1)S(1)}, bf16[16,56]{1,0:T(8,128)(2,1)S(1)}, u32[]{:S(2)}, u32[]{:S(2)}) collective-permute-start(bf16[16,56]{1,0:T(8,128)(2,1)S(1)} %bitcast.26), channel_id=1, source_target_pairs={{0,1},{1,0},{2,3},{3,2},{4,5},{5,4},{6,7},{7,6},{8,9},{9,8},{10,11... | collective-permute-start | bytes 5384 | tf_op jit(solution)/shard_map/ppermute | solution.py:198
  68.9 24.7 %collective-permute-start.18 = (bf16[448,1152]{1,0:T(8,128)(2,1)S(1)}, bf16[448,1152]{1,0:T(8,128)(2,1)}, u32[]{:S(2)}, u32[]{:S(2)}) collective-permute-start(bf16[448,1152]{1,0:T(8,128)(2,1)S(1)} %pad_maximum_fusion.1.refs_0_), channel_id=1, source_target_pairs={{0,8},{8,0},{16,24},{24,16},{32,40},{40,32},{48,56},{56,48},{64,72... | collective-permute-start | bytes 3096584 | tf_op jit(solution)/shard_map/ppermute | solution.py:134
  70.9 25.6 %collective-permute-start.17 = (bf16[448,1152]{1,0:T(8,128)(2,1)}, bf16[448,1152]{1,0:T(8,128)(2,1)}, u32[]{:S(2)}, u32[]{:S(2)}) collective-permute-start(bf16[448,1152]{1,0:T(8,128)(2,1)} %collective-permute-done.10.refs_0_), channel_id=1, source_target_pairs={{0,8},{8,0},{16,24},{24,16},{32,40},{40,32},{48,56},{56,48},{64,72... | collective-permute-start | bytes 3096584 | tf_op jit(solution)/shard_map/ppermute | solution.py:134
  77.7 22.1 %collective-permute-start.12 = (bf16[448,1152]{1,0:T(8,128)(2,1)}, bf16[448,1152]{1,0:T(8,128)(2,1)}, u32[]{:S(2)}, u32[]{:S(2)}) collective-permute-start(bf16[448,1152]{1,0:T(8,128)(2,1)} %collective-permute-done.11.refs_0_), channel_id=1, source_target_pairs={{0,16},{8,120},{16,32},{24,8},{32,48},{40,24},{48,64},{56,40},{64,... | collective-permute-start | bytes 3096584 | tf_op jit(solution)/shard_map/ppermute | solution.py:143
  78.8 4.0 %collective-permute-start.20 = (bf16[16,112]{1,0:T(8,128)(2,1)S(1)}, bf16[16,112]{1,0:T(8,128)(2,1)S(1)}, u32[]{:S(2)}, u32[]{:S(2)}) collective-permute-start(bf16[16,112]{1,0:T(8,128)(2,1)S(1)} %reshape.36), channel_id=1, source_target_pairs={{0,2},{1,3},{2,0},{3,1},{4,6},{5,7},{6,4},{7,5},{8,10},{9,11},{10,... | collective-permute-start | bytes 10760 | tf_op jit(solution)/shard_map/ppermute | solution.py:198
  82.7 28.3 %collective-permute-start.16 = (bf16[448,1152]{1,0:T(8,128)(2,1)}, bf16[448,1152]{1,0:T(8,128)(2,1)}, u32[]{:S(2)}, u32[]{:S(2)}) collective-permute-start(bf16[448,1152]{1,0:T(8,128)(2,1)} %collective-permute-done.4.refs_0_), channel_id=1, source_target_pairs={{0,8},{8,0},{16,24},{24,16},{32,40},{40,32},{48,56},{56,48},{64,72... | collective-permute-start | bytes 3096584 | tf_op jit(solution)/shard_map/ppermute | solution.py:134
  88.6 4.0 %collective-permute-start.21 = (bf16[16,224]{1,0:T(8,128)(2,1)S(1)}, bf16[16,224]{1,0:T(8,128)(2,1)S(1)}, u32[]{:S(2)}, u32[]{:S(2)}) collective-permute-start(bf16[16,224]{1,0:T(8,128)(2,1)S(1)} %reshape.37), channel_id=1, source_target_pairs={{0,4},{1,5},{2,6},{3,7},{4,0},{5,1},{6,2},{7,3},{8,12},{9,13},{10,... | collective-permute-start | bytes 21512 | tf_op jit(solution)/shard_map/ppermute | solution.py:198
  92.6 15.1 %collective-permute-start.8 = (bf16[320,1152]{1,0:T(8,128)(2,1)S(1)}, bf16[320,1152]{1,0:T(8,128)(2,1)}, u32[]{:S(2)}, u32[]{:S(2)}) collective-permute-start(bf16[320,1152]{1,0:T(8,128)(2,1)S(1)} %slice.31), channel_id=1, source_target_pairs={{0,16},{8,120},{16,32},{24,8},{32,48},{40,24},{48,64},{56,40},{64,... | collective-permute-start | bytes 2211848 | tf_op jit(solution)/shard_map/ppermute | solution.py:143
  93.6 42.8 %collective-permute-start.15 = (bf16[448,1152]{1,0:T(8,128)(2,1)}, bf16[448,1152]{1,0:T(8,128)(2,1)}, u32[]{:S(2)}, u32[]{:S(2)}) collective-permute-start(bf16[448,1152]{1,0:T(8,128)(2,1)} %collective-permute-done.11.refs_0_), channel_id=1, source_target_pairs={{0,8},{8,0},{16,24},{24,16},{32,40},{40,32},{48,56},{56,48},{64,72... | collective-permute-start | bytes 3096584 | tf_op jit(solution)/shard_map/ppermute | solution.py:134
  96.4 43.2 %collective-permute-start.14 = (bf16[448,1152]{1,0:T(8,128)(2,1)S(1)}, bf16[448,1152]{1,0:T(8,128)(2,1)}, u32[]{:S(2)}, u32[]{:S(2)}) collective-permute-start(bf16[448,1152]{1,0:T(8,128)(2,1)S(1)} %collective-permute-done.5.refs_0_), channel_id=1, source_target_pairs={{0,8},{8,0},{16,24},{24,16},{32,40},{40,32},{48,56},{56,48},{64,72... | collective-permute-start | bytes 3096584 | tf_op jit(solution)/shard_map/ppermute | solution.py:134
  99.8 44.2 %collective-permute-start.13 = (bf16[448,1152]{1,0:T(8,128)(2,1)}, bf16[448,1152]{1,0:T(8,128)(2,1)}, u32[]{:S(2)}, u32[]{:S(2)}) collective-permute-start(bf16[448,1152]{1,0:T(8,128)(2,1)} %collective-permute-done.12.refs_0_), channel_id=1, source_target_pairs={{0,8},{8,0},{16,24},{24,16},{32,40},{40,32},{48,56},{56,48},{64,72... | collective-permute-start | bytes 3096584 | tf_op jit(solution)/shard_map/ppermute | solution.py:134
  107.7 40.6 %collective-permute-start.9 = (bf16[320,1152]{1,0:T(8,128)(2,1)}, bf16[320,1152]{1,0:T(8,128)(2,1)}, u32[]{:S(2)}, u32[]{:S(2)}) collective-permute-start(bf16[320,1152]{1,0:T(8,128)(2,1)} %collective-permute-done.8.refs_0_), channel_id=1, source_target_pairs={{0,8},{8,0},{16,24},{24,16},{32,40},{40,32},{48,56},{56,48},{64,72... | collective-permute-start | bytes 2211848 | tf_op jit(solution)/shard_map/ppermute | solution.py:134
  111.1 6.1 %collective-permute-start.6 = (bf16[128,1152]{1,0:T(8,128)(2,1)}, bf16[128,1152]{1,0:T(8,128)(2,1)S(1)}, u32[]{:S(2)}, u32[]{:S(2)}) collective-permute-start(bf16[128,1152]{1,0:T(8,128)(2,1)} %slice.30), channel_id=1, source_target_pairs={{0,16},{8,120},{16,32},{24,8},{32,48},{40,24},{48,64},{56,40},{64,... | collective-permute-start | bytes 884744 | tf_op jit(solution)/shard_map/ppermute | solution.py:143
  117.1 33.8 %collective-permute-start.7 = (bf16[128,1152]{1,0:T(8,128)(2,1)S(1)}, bf16[128,1152]{1,0:T(8,128)(2,1)S(1)}, u32[]{:S(2)}, u32[]{:S(2)}) collective-permute-start(bf16[128,1152]{1,0:T(8,128)(2,1)S(1)} %collective-permute-done.6.refs_0_), channel_id=1, source_target_pairs={{0,8},{8,0},{16,24},{24,16},{32,40},{40,32},{48,56},{56,48},{64,72... | collective-permute-start | bytes 884744 | tf_op jit(solution)/shard_map/ppermute | solution.py:134
  120.0 1.2 copy-start.1

commit v3 on v2

--- a/solution.py
+++ b/solution.py
@@ -8,9 +8,9 @@
 SITE_ROWS = ("site", "rows")
 SITE_ROWS_WIDTH = ("site", "rows", "width")
 SITE_WIDTH = ("site", "width")
-EARLY = (144, 112)
-CUTS = (0, 144, 256, 448)
-LAST = 128
+EARLY = (128, 112)
+CUTS = (0, 128, 240, 448)
+LAST = 96
 
 
 def spread(row, lane, count):
@@ -32,8 +32,8 @@
     def kernel(*refs):
         share_ref, refs = refs[0], refs[1:]
         array_refs, refs = refs[: len(arrays)], refs[len(arrays) :]
-        train_ref, step_ref, *whole_refs, top_ref = refs[:6]
-        refs = refs[6:]
+        train_ref, step_ref, *whole_refs, top_ref = refs[:5]
+        refs = refs[5:]
         share_buf, array_bufs, gain_bufs = refs[0], refs[1 : 1 + len(arrays)], refs[1 + len(arrays) : 3 + len(arrays)]
         sems, small_sems = refs[-2:]
         small = [
@@ -68,7 +68,8 @@
             for k, w in enumerate(widths):
                 whole = column * array_bufs[2 * k][low:high, :] + rest * array_bufs[2 * k + 1][low:high, :]
                 piece = max(p for p in range(3) if starts[p] <= low)
-                whole_refs[piece][low - starts[piece] : high - starts[piece], at : at + w] = whole
+                if piece < 2:
+                    whole_refs[piece][low - starts[piece] : high - starts[piece], at : at + w] = whole
                 top = jnp.max(jnp.abs(whole), axis=0, keepdims=True)
                 tops[k] = top if c == 0 else jnp.maximum(tops[k], top)
                 at += w
@@ -81,8 +82,8 @@
     return pl.pallas_call(
         kernel,
         in_specs=[pl.BlockSpec(memory_space=pltpu.HBM)] * len(inputs),
-        out_specs=[pl.BlockSpec(memory_space=pltpu.VMEM)] * 4,
-        out_shape=[jax.ShapeDtypeStruct((b - a, total), jnp.float32) for a, b in zip(starts, starts[1:])]
+        out_specs=[pl.BlockSpec(memory_space=pltpu.VMEM)] * 3,
+        out_shape=[jax.ShapeDtypeStruct((b - a, total), jnp.float32) for a, b in zip(starts, starts[1:3])]
         + [jax.ShapeDtypeStruct((n, 1, wide), jnp.float32)],
         scratch_shapes=[pltpu.VMEM((1, depth), jnp.float32)]
         + [pltpu.VMEM(a.shape, jnp.float32) for a in arrays]
@@ -93,40 +94,40 @@
     )(*inputs)
 
 
-def place(outs, block, hops, flip, skip, depth, shapes):
+def place(outs, blocks, depth, shapes):
     n = lax.axis_size("rows")
     ends = [0]
     for shape in shapes:
         ends.append(ends[-1] + shape[1])
-    rows = block.shape[0]
 
     def kernel(*refs):
-        block_ref, out_refs, sems = refs[0], refs[-1 - len(shapes) : -1], refs[-1]
+        block_refs, out_refs, sems = refs[: len(blocks)], refs[-1 - len(shapes) : -1], refs[-1]
         me = lax.axis_index("rows")
         core = me & 1
-        owner = ((me - core - (2 - 4 * core) * hops) & (n - 1)) + (core ^ flip)
-        at = pl.multiple_of(owner * depth + skip, 32)
-        copies = [
-            pltpu.make_async_copy(block_ref.at[:, b:e], out.at[pl.ds(at, rows), :], sems.at[k])
-            for k, (out, b, e) in enumerate(zip(out_refs, ends, ends[1:]))
-        ]
-        for copy in copies:
-            copy.start()
+        copies = []
+        for i, (block_ref, (block, hops, flip, skip)) in enumerate(zip(block_refs, blocks)):
+            owner = ((me - core - (2 - 4 * core) * hops) & (n - 1)) + (core ^ flip)
+            at = pl.multiple_of(owner * depth + skip, 32)
+            for k, (out, b, e) in enumerate(zip(out_refs, ends, ends[1:])):
+                to = out.at[pl.ds(at, block.shape[0]), :]
+                copies.append(pltpu.make_async_copy(block_ref.at[:, b:e], to, sems.at[i, k]))
+                copies[-1].start()
         for copy in copies:
             copy.wait()
 
     anywhere = [pl.BlockSpec(memory_space=pltpu.HBM)] * len(shapes)
     given = [] if outs is None else list(outs)
+    size = sum(block.size for block, *_ in blocks)
     return pl.pallas_call(
         kernel,
-        in_specs=[pl.BlockSpec(memory_space=pltpu.VMEM)] + anywhere[: len(given)],
+        in_specs=[pl.BlockSpec(memory_space=pltpu.VMEM)] * len(blocks) + anywhere[: len(given)],
         out_specs=anywhere,
         out_shape=[jax.ShapeDtypeStruct(shape, jnp.bfloat16) for shape in shapes],
-        input_output_aliases={1 + k: k for k in range(len(given))},
-        scratch_shapes=[pltpu.SemaphoreType.DMA((len(shapes),))],
+        input_output_aliases={len(blocks) + k: k for k in range(len(given))},
+        scratch_shapes=[pltpu.SemaphoreType.DMA((len(blocks), len(shapes)))],
         compiler_params=pltpu.CompilerParams(vmem_limit_bytes=4 << 20),
-        cost_estimate=pl.CostEstimate(flops=2 * block.size, bytes_accessed=4 * block.size, transcendentals=0),
-    )(block, *given)
+        cost_estimate=pl.CostEstimate(flops=2 * size, bytes_accessed=4 * size, transcendentals=0),
+    )(*[block for block, *_ in blocks], *given)
 
 
 def partner(array):
@@ -150,7 +151,7 @@
     pairs = [(one_query, other_query), (one_key, other_key), (one_value, other_value)]
     widths = [one.shape[1] for one, _ in pairs]
     ends = [0, widths[0], widths[0] + widths[1], sum(widths)]
-    *early, late, tops = mixed(mix_share, pairs, (norm_train, norm_step), n)
+    *early, tops = mixed(mix_share, pairs, (norm_train, norm_step), n)
     coming = [onward(early[0]), onward(early[1])]
     seen = lax.all_to_all(tops, "rows", split_axis=0, concat_axis=0, tiled=True)
     scale = seen.max(axis=(0, 1))
@@ -161,19 +162,22 @@
     def scaled(whole):
         return lax.optimization_barrier((whole / scale).astype(jnp.bfloat16))
 
+    share = mix_share[sum(EARLY) :, None]
+    late = [share * one[sum(EARLY) :] + (1.0 - share) * other[sum(EARLY) :] for one, other in pairs]
+    late = lax.optimization_barrier(jnp.concatenate(late, axis=1))
     mine_b = scaled(late)
     *early, mine_b, scale = lax.optimization_barrier((*early, mine_b, scale))
     mine = jnp.concatenate([(a / scale).astype(jnp.bfloat16) for a in early] + [mine_b], axis=0)
     shapes = [(n * depth, w) for w in widths]
 
-    def put(outs, block, hops, flip, skip=0):
-        return place(outs, block, hops, flip, skip, depth, shapes)
-
-    outs = put(None, mine, 0, 0)
+    def put(outs, *blocks):
+        return place(outs, blocks, depth, shapes)
+
+    outs = put(None, (mine, 0, 0, 0))
     sibling = partner(mine)
     *coming, scale_in, _ = lax.optimization_barrier((*coming, scale, sibling))
     come = [(a / scale_in).astype(jnp.bfloat16) for a in coming]
-    outs = put(outs, sibling, 0, 1)
+    outs = put(outs, (sibling, 0, 1, 0))
     units = [mine, sibling]
     steps = n // 2 - 1
     for step in range(1, steps + 1):
@@ -188,9 +192,13 @@
                 here = jnp.concatenate([*come, here], axis=0)
             else:
                 here = onward(units[step - 1][low:high])
-            outs = put(outs, here, hop, chain, low)
             across = partner(here)
-            outs = put(outs, across, -hop, 1 ^ chain, low)
+            direct, crossed = (here, hop, chain, low), (across, -hop, 1 ^ chain, low)
+            if k > steps:
+                outs = put(outs, direct, crossed)
+            else:
+                outs = put(outs, direct)
+                outs = put(outs, crossed)
         units.append(here)
 
     k, turn = 1, 1

time: 153 us -> 151 us (0.987)
  blocking collectives: 18.2 us -> 0 us
  waiting for transfers between devices: 61.9 us -> 71.1 us
  starting transfers between devices: 29.9 us -> 34.6 us
  other arithmetic: 1.69 us -> 4 us
    all_to_all x1 -> x0, blocking collectives: 18.2 us -> none  [body(): seen = lax.all_to_all(tops, 'rows', split_axis=0, concat_axis=0, tiled=True)]
    all_to_all x0 -> x1, starting transfers between devices: none -> 9.98 us  [body(): seen = lax.all_to_all(tops, 'rows', split_axis=0, concat_axis=0, tiled=True)]
    ppermute x9, starting transfers between devices: 15.2 us -> 10.4 us  [partner(): return lax.ppermute(array, 'rows', [(i, i ^ 1) for i in range(n)])]
    all_to_all x0 -> x1, waiting for transfers between devices: none -> 4.59 us  [body(): seen = lax.all_to_all(tops, 'rows', split_axis=0, concat_axis=0, tiled=True)]
    ppermute x10, waiting for transfers between devices: 59.6 us -> 64.2 us  [onward(): return lax.ppermute(array, 'rows', [(i, to(i)) for i in range(n)])]
    add x0 -> x2, other arithmetic: none -> 2.66 us  [body(): share * one[sum(EARLY):] + (1.0 - share) * other[sum(EARLY):]]
    pallas_call x18 -> x17, Pallas kernels: 31.4 us -> 30.8 us  [place(): pl.pallas_call(kernel, in_specs=[pl.BlockSpec(memory_space=pltpu.VMEM)] *...]
  transfers between devices with their start and end apart: 22 -> 23, of which waited for: 11 -> 12; matrix products, arithmetic and copies ran while one was open for 2% -> 4% of each run, Pallas kernels for 20% -> 20%
where the time goes in v3:
time: 151 us; the launch traced here: 150 us
  waiting for transfers between devices  71.1 us (47%)
  starting transfers between devices  34.6 us (23%)
  Pallas kernels  34.2 us (23%)
  local copies, waits for them, and re-layouts  5.08 us (3%)
  other arithmetic  4 us (3%)
    ppermute x10, waiting for transfers between devices, onward(): return lax.ppermute(array, 'rows', [(i, to(i)) for i in range(n)])  64.2 us
    pallas_call x17, Pallas kernels, place(): pl.pallas_call(kernel, in_specs=[pl.BlockSpec(memory_space=pltpu.VMEM)] *...  30.8 us
    ppermute x9, starting transfers between devices, partner(): return lax.ppermute(array, 'rows', [(i, i ^ 1) for i in range(n)])  10.4 us
    all_to_all x1, starting transfers between devices, body(): seen = lax.all_to_all(tops, 'rows', split_axis=0, concat_axis=0, tiled=True)  9.98 us
    ppermute x10, starting transfers between devices, onward(): return lax.ppermute(array, 'rows', [(i, to(i)) for i in range(n)])  7.23 us
    ppermute x3, starting transfers between devices, body(): other = lax.ppermute(norms, 'width', [(i, i ^ k) for i in range(wide)])  6.99 us
    all_to_all x1, waiting for transfers between devices, body(): seen = lax.all_to_all(tops, 'rows', split_axis=0, concat_axis=0, tiled=True)  4.59 us
    pallas_call x1, Pallas kernels, mixed(): pl.pallas_call(kernel, in_specs=[pl.BlockSpec(memory_space=pltpu.HBM)] *...  3.38 us
  transfers between devices with their start and end apart: 23, of which 12 were waited for; matrix products, arithmetic and copies ran while one was open for 4% of the time, Pallas kernels for 20%

profile of v3, /device:TPU:1, one launch (start us, length us, event | category | flops | bytes accessed | tf_op | source)
XLA Modules:
  0.0 150.1 jit_solution(12392373939993291552)
XLA Ops:
  0.6 3.4 %shard_map.144 = (f32[128,1152]{1,0:T(8,128)}, f32[112,1152]{1,0:T(8,128)}, f32[16,1,1208]{2,1,0:T(1,128)}) custom-call(f32[1,448]{1,0:T(1,128)} %bitcast.26, f32[448,896]{1,0:T(8,128)} %refs_1_.1, f32[448,896]{1,0:T(8,128)} %refs_2_.1, f32[448,128]{1,0:T(8,128)} %refs_3_.1, f32[448,128]{1,0:T(8,128)} %refs_4_.1, f32[448,128]{1,0:T(8,128)} %refs_5_.1, ...), custom_call_target="tpu_custom_call" | custom-call | flops 3096576 | bytes 6193152 | tf_op jit(solution)/shard_map/pallas_call | solution.py:82
  4.0 10.0 %all-to-all-start = ((f32[16,1,1208]{2,1,0:T(1,128)}), f32[16,1,1208]{2,1,0:T(1,128)S(1)}, u32[]{:S(2)}, u32[]{:S(2)}) async-start(f32[16,1,1208]{2,1,0:T(1,128)} %get-tuple-element.70), calls=%async_computation | async-start | bytes 163840 | tf_op jit(solution)/shard_map/all_to_all | solution.py:156
  14.8 1.2 multiply_add_fusion.2
  15.9 1.5 multiply_add_fusion
  17.5 4.6 %all-to-all-done = f32[16,1,1208]{2,1,0:T(1,128)S(1)} async-done(((f32[16,1,1208]{2,1,0:T(1,128)}), f32[16,1,1208]{2,1,0:T(1,128)S(1)}, u32[]{:S(2)}, u32[]{:S(2)}) %all-to-all-start) | async-done | bytes 77344 | tf_op jit(solution)/shard_map/all_to_all | solution.py:156
  24.5 13.4 %collective-permute-done.1 = f32[112,1152]{1,0:T(8,128)S(1)} collective-permute-done((f32[112,1152]{1,0:T(8,128)S(1)}, f32[112,1152]{1,0:T(8,128)S(1)}, u32[]{:S(2)}, u32[]{:S(2)}) %collective-permute-start.1) | collective-permute-done | bytes 516128 | tf_op jit(solution)/shard_map/ppermute | solution.py:144
  38.0 1.1 collective-permute-start.10
  39.1 4.0 %collective-permute-done.3 = bf16[208,1152]{1,0:T(8,128)(2,1)S(1)} collective-permute-done((bf16[208,1152]{1,0:T(8,128)(2,1)S(1)}, bf16[208,1152]{1,0:T(8,128)(2,1)S(1)}, u32[]{:S(2)}, u32[]{:S(2)}) %collective-permute-start.3) | collective-permute-done | bytes 479264 | tf_op jit(solution)/shard_map/ppermute | solution.py:144
  43.1 1.1 collective-permute-start.4
  44.2 10.0 %collective-permute-done.10.refs_0_ = bf16[448,1152]{1,0:T(8,128)(2,1)} collective-permute-done((bf16[448,1152]{1,0:T(8,128)(2,1)S(1)}, bf16[448,1152]{1,0:T(8,128)(2,1)}, u32[]{:S(2)}, u32[]{:S(2)}) %collective-permute-start.10) | collective-permute-done | bytes 1032224 | tf_op jit(solution)/shard_map/ppermute | solution.py:144
  54.2 1.0 collective-permute-start.11
  55.2 10.1 %collective-permute-done.4.refs_0_ = bf16[448,1152]{1,0:T(8,128)(2,1)} collective-permute-done((bf16[448,1152]{1,0:T(8,128)(2,1)S(1)}, bf16[448,1152]{1,0:T(8,128)(2,1)}, u32[]{:S(2)}, u32[]{:S(2)}) %collective-permute-start.4) | collective-permute-done | bytes 1032224 | tf_op jit(solution)/shard_map/ppermute | solution.py:144
  65.3 1.0 collective-permute-start.5
  66.3 1.3 collective-permute-start.19
  67.5 1.4 collective-permute-start.18
  68.9 7.4 %collective-permute-done.11.refs_0_ = bf16[448,1152]{1,0:T(8,128)(2,1)} collective-permute-done((bf16[448,1152]{1,0:T(8,128)(2,1)}, bf16[448,1152]{1,0:T(8,128)(2,1)}, u32[]{:S(2)}, u32[]{:S(2)}) %collective-permute-start.11) | collective-permute-done | bytes 1032224 | tf_op jit(solution)/shard_map/ppermute | solution.py:144
  76.3 1.0 collective-permute-start.12
  77.4 2.8 %collective-permute-start.20 = (bf16[16,112]{1,0:T(8,128)(2,1)S(1)}, bf16[16,112]{1,0:T(8,128)(2,1)S(1)}, u32[]{:S(2)}, u32[]{:S(2)}) collective-permute-start(bf16[16,112]{1,0:T(8,128)(2,1)S(1)} %reshape.39), channel_id=1, source_target_pairs={{0,2},{1,3},{2,0},{3,1},{4,6},{5,7},{6,4},{7,5},{8,10},{9,11},{10,... | collective-permute-start | bytes 10760 | tf_op jit(solution)/shard_map/ppermute | solution.py:206
  80.2 1.2 collective-permute-done.20
  81.4 5.9 %collective-permute-done.5.refs_0_ = bf16[448,1152]{1,0:T(8,128)(2,1)S(1)} collective-permute-done((bf16[448,1152]{1,0:T(8,128)(2,1)}, bf16[448,1152]{1,0:T(8,128)(2,1)S(1)}, u32[]{:S(2)}, u32[]{:S(2)}) %collective-permute-start.5) | collective-permute-done | bytes 1032224 | tf_op jit(solution)/shard_map/ppermute | solution.py:144
  87.3 0.9 slice.59
  88.2 1.0 collective-permute-start.8
  89.3 2.9 %collective-permute-start.21 = (bf16[16,224]{1,0:T(8,128)(2,1)S(1)}, bf16[16,224]{1,0:T(8,128)(2,1)S(1)}, u32[]{:S(2)}, u32[]{:S(2)}) collective-permute-start(bf16[16,224]{1,0:T(8,128)(2,1)S(1)} %reshape.40), channel_id=1, source_target_pairs={{0,4},{1,5},{2,6},{3,7},{4,0},{5,1},{6,2},{7,3},{8,12},{9,13},{10,... | collective-permute-start | bytes 21512 | tf_op jit(solution)/shard_map/ppermute | solution.py:206
  92.2 1.1 collective-permute-done.21
  93.3 2.2 %collective-permute-start.16 = (bf16[448,1152]{1,0:T(8,128)(2,1)}, bf16[448,1152]{1,0:T(8,128)(2,1)}, u32[]{:S(2)}, u32[]{:S(2)}) collective-permute-start(bf16[448,1152]{1,0:T(8,128)(2,1)} %collective-permute-done.4.refs_0_), channel_id=1, source_target_pairs={{0,8},{8,0},{16,24},{24,16},{32,40},{40,32},{48,56},{56,48},{64,72... | collective-permute-start | bytes 3096584 | tf_op jit(solution)/shard_map/ppermute | solution.py:135
  96.1 2.3 %collective-permute-done.12.refs_0_ = bf16[448,1152]{1,0:T(8,128)(2,1)} collective-permute-done((bf16[448,1152]{1,0:T(8,128)(2,1)}, bf16[448,1152]{1,0:T(8,128)(2,1)}, u32[]{:S(2)}, u32[]{:S(2)}) %collective-permute-start.12) | collective-permute-done | bytes 1032224 | tf_op jit(solution)/shard_map/ppermute | solution.py:144
  98.4 2.1 %collective-permute-start.13 = (bf16[448,1152]{1,0:T(8,128)(2,1)}, bf16[448,1152]{1,0:T(8,128)(2,1)}, u32[]{:S(2)}, u32[]{:S(2)}) collective-permute-start(bf16[448,1152]{1,0:T(8,128)(2,1)} %collective-permute-done.12.refs_0_), channel_id=1, source_target_pairs={{0,8},{8,0},{16,24},{24,16},{32,40},{40,32},{48,56},{56,48},{64,72... | collective-permute-start | bytes 3096584 | tf_op jit(solution)/shard_map/ppermute | solution.py:135
  100.5 6.6 %collective-permute-done.8.refs_0_ = bf16[352,1152]{1,0:T(8,128)(2,1)} collective-permute-done((bf16[352,1152]{1,0:T(8,128)(2,1)}, bf16[352,1152]{1,0:T(8,128)(2,1)}, u32[]{:S(2)}, u32[]{:S(2)}) %collective-permute-start.8) | collective-permute-done | bytes 811040 | tf_op jit(solution)/shard_map/ppermute | solution.py:144
  107.1 2.1 %collective-permute-start.9 = (bf16[352,1152]{1,0:T(8,128)(2,1)}, bf16[352,1152]{1,0:T(8,128)(2,1)}, u32[]{:S(2)}, u32[]{:S(2)}) collective-permute-start(bf16[352,1152]{1,0:T(8,128)(2,1)} %collective-permute-done.8.refs_0_), channel_id=1, source_target_pairs={{0,8},{8,0},{16,24},{24,16},{32,40},{40,32},{48,56},{56,48},{64,72... | collective-permute-start | bytes 2433032 | tf_op jit(solution)/shard_map/ppermute | solution.py:135
  109.8 1.0 shard_map.145
  111.4 4.5 %collective-permute-done.6.refs_0_ = bf16[96,1152]{1,0:T(8,128)(2,1)S(1)} collective-permute-done((bf16[96,1152]{1,0:T(8,128)(2,1)S(1)}, bf16[96,1152]{1,0:T(8,128)(2,1)S(1)}, u32[]{:S(2)}, u32[]{:S(2)}) %collective-permute-start.6) | collective-permute-done | bytes 221216 | tf_op jit(solution)/shard_map/ppermute | solution.py:144
  116.0 2.1 %collective-permute-start.7 = (bf16[96,1152]{1,0:T(8,128)(2,1)S(1)}, bf16[96,1152]{1,0:T(8,128)(2,1)S(1)}, u32[]{:S(2)}, u32[]{:S(2)}) collective-permute-start(bf16[96,1152]{1,0:T(8,128)(2,1)S(1)} %collective-permute-done.6.refs_0_), channel_id=1, source_target_pairs={{0,8},{8,0},{16,24},{24,16},{32,40},{40,32},{48,56},{56,48},{64,72... | collective-permute-start | bytes 663560 | tf_op jit(solution)/shard_map/ppermute | solution.py:135
  118.8 1.2 copy-done.1
  120.0 1.0 shard_map.146
  121.0 1.0 shard_map.147
  122.0 2.2 %shard_map.148 = (bf16[7168,896]{1,0:T(8,128)(2,1)}, bf16[7168,128]{1,0:T(8,128)(2,1)}, bf16[7168,128]{1,0:T(8,128)(2,1)}) custom-call(bf16[448,1152]{1,0:T(8,128)(2,1)} %collective-permute-done.18.refs_0_, bf16[7168,896]{1,0:T(8,128)(2,1)} %get-tuple-element.84.refs_1_, ...), custom_call_target="tpu_custom_call", output_to_operand_aliasing={{0}: (1, {}), {1}: (2, {}), {2}: (3, {})} | custom-call | flops 1032192 | bytes 2064384 | tf_op jit(solution)/shard_map/pallas_call | solution.py:121
  124.2 2.2 %shard_map.149 = (bf16[7168,896]{1,0:T(8,128)(2,1)}, bf16[7168,128]{1,0:T(8,128)(2,1)}, bf16[7168,128]{1,0:T(8,128)(2,1)}) custom-call(bf16[448,1152]{1,0:T(8,128)(2,1)} %collective-permute-done.10.refs_0_, bf16[7168,896]{1,0:T(8,128)(2,1)} %get-tuple-element.87.refs_1_, ...), custom_call_target="tpu_custom_call", output_to_operand_aliasing={{0}: (1, {}), {1}: (2, {}), {2}: (3, {})} | custom-call | flops 1032192 | bytes 2064384 | tf_op jit(solution)/shard_map/pallas_call | solution.py:121
  126.4 2.2 %shard_map.150 = (bf16[7168,896]{1,0:T(8,128)(2,1)}, bf16[7168,128]{1,0:T(8,128)(2,1)}, bf16[7168,128]{1,0:T(8,128)(2,1)}) custom-call(bf16[448,1152]{1,0:T(8,128)(2,1)} %collective-permute-done.17.refs_0_, bf16[7168,896]{1,0:T(8,128)(2,1)} %get-tuple-element.90.refs_1_, ...), custom_call_target="tpu_custom_call", output_to_operand_aliasing={{0}: (1, {}), {1}: (2, {}), {2}: (3, {})} | custom-call | flops 1032192 | bytes 2064384 | tf_op jit(solution)/shard_map/pallas_call | solution.py:121
  128.6 2.2 %shard_map.151 = (bf16[7168,896]{1,0:T(8,128)(2,1)}, bf16[7168,128]{1,0:T(8,128)(2,1)}, bf16[7168,128]{1,0:T(8,128)(2,1)}) custom-call(bf16[448,1152]{1,0:T(8,128)(2,1)} %collective-permute-done.4.refs_0_, bf16[7168,896]{1,0:T(8,128)(2,1)} %get-tuple-element.93.refs_1_, ...), custom_call_target="tpu_custom_call", output_to_operand_aliasing={{0}: (1, {}), {1}: (2, {}), {2}: (3, {})} | custom-call | flops 1032192 | bytes 2064384 | tf_op jit(solution)/shard_map/pallas_call | solution.py:121
  130.8 2.2 %shard_map.152 = (bf16[7168,896]{1,0:T(8,128)(2,1)}, bf16[7168,128]{1,0:T(8,128)(2,1)}, bf16[7168,128]{1,0:T(8,128)(2,1)}) custom-call(bf16[448,1152]{1,0:T(8,128)(2,1)} %collective-permute-done.16.refs_0_, bf16[7168,896]{1,0:T(8,128)(2,1)} %get-tuple-element.96.refs_1_, ...), custom_call_target="tpu_custom_call", output_to_operand_aliasing={{0}: (1, {}), {1}: (2, {}), {2}: (3, {})} | custom-call | flops 1032192 | bytes 2064384 | tf_op jit(solution)/shard_map/pallas_call | solution.py:121
  133.0 2.2 %shard_map.153 = (bf16[7168,896]{1,0:T(8,128)(2,1)}, bf16[7168,128]{1,0:T(8,128)(2,1)}, bf16[7168,128]{1,0:T(8,128)(2,1)}) custom-call(bf16[448,1152]{1,0:T(8,128)(2,1)} %collective-permute-done.11.refs_0_, bf16[7168,896]{1,0:T(8,128)(2,1)} %get-tuple-element.99.refs_1_, ...), custom_call_target="tpu_custom_call", output_to_operand_aliasing={{0}: (1, {}), {1}: (2, {}), {2}: (3, {})} | custom-call | flops 1032192 | bytes 2064384 | tf_op jit(solution)/shard_map/pallas_call | solution.py:121
  135.2 2.2 %shard_map.154 = (bf16[7168,896]{1,0:T(8,128)(2,1)}, bf16[7168,128]{1,0:T(8,128)(2,1)}, bf16[7168,128]{1,0:T(8,128)(2,1)}) custom-call(bf16[448,1152]{1,0:T(8,128)(2,1)} %collective-permute-done.15.refs_0_, bf16[7168,896]{1,0:T(8,128)(2,1)} %get-tuple-element.102.refs_1_, ...), custom_call_target="tpu_custom_call", output_to_operand_aliasing={{0}: (1, {}), {1}: (2, {}), {2}: (3, {})} | custom-call | flops 1032192 | bytes 2064384 | tf_op jit(solution)/shard_map/pallas_call | solution.py:121
  137.4 1.0 shard_map.155
  138.4 2.2 %shard_map.156 = (bf16[7168,896]{1,0:T(8,128)(2,1)}, bf16[7168,128]{1,0:T(8,128)(2,1)}, bf16[7168,128]{1,0:T(8,128)(2,1)}) custom-call(bf16[448,1152]{1,0:T(8,128)(2,1)} %collective-permute-done.14.refs_0_, bf16[7168,896]{1,0:T(8,128)(2,1)} %get-tuple-element.108.refs_1_, ...), custom_call_target="tpu_custom_call", output_to_operand_aliasing={{0}: (1, {}), {1}: (2, {}), {2}: (3, {})} | custom-call | flops 1032192 | bytes 2064384 | tf_op jit(solution)/shard_map/pallas_call | solution.py:121
  140.6 2.2 %shard_map.157 = (bf16[7168,896]{1,0:T(8,128)(2,1)}, bf16[7168,128]{1,0:T(8,128)(2,1)}, bf16[7168,128]{1,0:T(8,128)(2,1)}) custom-call(bf16[448,1152]{1,0:T(8,128)(2,1)} %collective-permute-done.12.refs_0_, bf16[7168,896]{1,0:T(8,128)(2,1)} %get-tuple-element.111.refs_1_, ...), custom_call_target="tpu_custom_call", output_to_operand_aliasing={{0}: (1, {}), {1}: (2, {}), {2}: (3, {})} | custom-call | flops 1032192 | bytes 2064384 | tf_op jit(solution)/shard_map/pallas_call | solution.py:121
  142.8 2.2 %shard_map.158 = (bf16[7168,896]{1,0:T(8,128)(2,1)}, bf16[7168,128]{1,0:T(8,128)(2,1)}, bf16[7168,128]{1,0:T(8,128)(2,1)}) custom-call(bf16[448,1152]{1,0:T(8,128)(2,1)} %collective-permute-done.13.refs_0_, bf16[7168,896]{1,0:T(8,128)(2,1)} %get-tuple-element.114.refs_1_, ...), custom_call_target="tpu_custom_call", output_to_operand_aliasing={{0}: (1, {}), {1}: (2, {}), {2}: (3, {})} | custom-call | flops 1032192 | bytes 2064384 | tf_op jit(solution)/shard_map/pallas_call | solution.py:121
  145.0 2.0 %shard_map.159 = (bf16[7168,896]{1,0:T(8,128)(2,1)}, bf16[7168,128]{1,0:T(8,128)(2,1)}, bf16[7168,128]{1,0:T(8,128)(2,1)}) custom-call(bf16[352,1152]{1,0:T(8,128)(2,1)} %collective-permute-done.8.refs_0_, bf16[7168,896]{1,0:T(8,128)(2,1)} %get-tuple-element.117.refs_1_, ...), custom_call_target="tpu_custom_call", output_to_operand_aliasing={{0}: (1, {}), {1}: (2, {}), {2}: (3, {})} | custom-call | flops 811008 | bytes 1622016 | tf_op jit(solution)/shard_map/pallas_call | solution.py:121
  147.1 2.0 %shard_map.160 = (bf16[7168,896]{1,0:T(8,128)(2,1)}, bf16[7168,128]{1,0:T(8,128)(2,1)}, bf16[7168,128]{1,0:T(8,128)(2,1)}) custom-call(bf16[352,1152]{1,0:T(8,128)(2,1)} %collective-permute-done.9.refs_0_, bf16[7168,896]{1,0:T(8,128)(2,1)} %get-tuple-element.120.refs_1_, ...), custom_call_target="tpu_custom_call", output_to_operand_aliasing={{0}: (1, {}), {1}: (2, {}), {2}: (3, {})} | custom-call | flops 811008 | bytes 1622016 | tf_op jit(solution)/shard_map/pallas_call | solution.py:121
  (58 shorter events, 6.9 us)
Async XLA Ops:
  4.0 18.1 %all-to-all-start = ((f32[16,1,1208]{2,1,0:T(1,128)}), f32[16,1,1208]{2,1,0:T(1,128)S(1)}, u32[]{:S(2)}, u32[]{:S(2)}) async-start(f32[16,1,1208]{2,1,0:T(1,128)} %get-tuple-element.70), calls=%async_computation | async-start | bytes 163840 | tf_op jit(solution)/shard_map/all_to_all | solution.py:156
  17.4 4.8 %copy-start.2 = (f32[128,1152]{1,0:T(8,128)S(1)}, f32[128,1152]{1,0:T(8,128)}, u32[]{:S(2)}) copy-start(f32[128,1152]{1,0:T(8,128)} %get-tuple-element.72) | copy-start | bytes 1769476
  17.5 4.9 %copy-start.4 = (f32[112,1152]{1,0:T(8,128)S(1)}, f32[112,1152]{1,0:T(8,128)}, u32[]{:S(2)}) copy-start(f32[112,1152]{1,0:T(8,128)} %get-tuple-element.73) | copy-start | bytes 1548292
  22.3 1.1 copy-start.3
  22.3 1.2 copy-start.5
  22.5 15.4 %collective-permute-start.2 = (bf16[448,1152]{1,0:T(8,128)(2,1)S(1)}, bf16[448,1152]{1,0:T(8,128)(2,1)S(1)}, u32[]{:S(2)}, u32[]{:S(2)}) collective-permute-start(bf16[448,1152]{1,0:T(8,128)(2,1)S(1)} %pad_maximum_fusion.refs_0_), channel_id=1, source_target_pairs={{0,8},{8,0},{16,24},{24,16},{32,40},{40,32},{48,56},{56,48},{64,72... | collective-permute-start | bytes 3096584 | tf_op jit(solution)/shard_map/ppermute | solution.py:135
  23.3 14.6 %collective-permute-start = (f32[128,1152]{1,0:T(8,128)S(1)}, f32[128,1152]{1,0:T(8,128)S(1)}, u32[]{:S(2)}, u32[]{:S(2)}) collective-permute-start(f32[128,1152]{1,0:T(8,128)S(1)} %copy-done.3), channel_id=1, source_target_pairs={{0,16},{8,120},{16,32},{24,8},{32,48},{40,24},{48,64},{56,40},{64,... | collective-permute-start | bytes 1769480 | tf_op jit(solution)/shard_map/ppermute | solution.py:144
  23.5 14.4 %collective-permute-start.1 = (f32[112,1152]{1,0:T(8,128)S(1)}, f32[112,1152]{1,0:T(8,128)S(1)}, u32[]{:S(2)}, u32[]{:S(2)}) collective-permute-start(f32[112,1152]{1,0:T(8,128)S(1)} %copy-done.5), channel_id=1, source_target_pairs={{0,16},{8,120},{16,32},{24,8},{32,48},{40,24},{48,64},{56,40},{64,... | collective-permute-start | bytes 1548296 | tf_op jit(solution)/shard_map/ppermute | solution.py:144
  23.9 19.2 %collective-permute-start.3 = (bf16[208,1152]{1,0:T(8,128)(2,1)S(1)}, bf16[208,1152]{1,0:T(8,128)(2,1)S(1)}, u32[]{:S(2)}, u32[]{:S(2)}) collective-permute-start(bf16[208,1152]{1,0:T(8,128)(2,1)S(1)} %divide_convert_fusion), channel_id=1, source_target_pairs={{0,16},{8,120},{16,32},{24,8},{32,48},{40,24},{48,64},{56,40},{64,... | collective-permute-start | bytes 1437704 | tf_op jit(solution)/shard_map/ppermute | solution.py:144
  37.9 5.2 %copy-start = (bf16[448,1152]{1,0:T(8,128)(2,1)}, bf16[448,1152]{1,0:T(8,128)(2,1)S(1)}, u32[]{:S(2)}) copy-start(bf16[448,1152]{1,0:T(8,128)(2,1)S(1)} %collective-permute-done.2.refs_0_) | copy-start | bytes 3096580
  38.0 16.2 %collective-permute-start.10 = (bf16[448,1152]{1,0:T(8,128)(2,1)S(1)}, bf16[448,1152]{1,0:T(8,128)(2,1)}, u32[]{:S(2)}, u32[]{:S(2)}) collective-permute-start(bf16[448,1152]{1,0:T(8,128)(2,1)S(1)} %collective-permute-done.2.refs_0_), channel_id=1, source_target_pairs={{0,16},{8,120},{16,32},{24,8},{32,48},{40,24},{48,64},{56,40},{64,... | collective-permute-start | bytes 3096584 | tf_op jit(solution)/shard_map/ppermute | solution.py:144
  43.1 22.1 %collective-permute-start.4 = (bf16[448,1152]{1,0:T(8,128)(2,1)S(1)}, bf16[448,1152]{1,0:T(8,128)(2,1)}, u32[]{:S(2)}, u32[]{:S(2)}) collective-permute-start(bf16[448,1152]{1,0:T(8,128)(2,1)S(1)} %pad_maximum_fusion.1.refs_0_), channel_id=1, source_target_pairs={{0,16},{8,120},{16,32},{24,8},{32,48},{40,24},{48,64},{56,40},{64,... | collective-permute-start | bytes 3096584 | tf_op jit(solution)/shard_map/ppermute | solution.py:144
  54.2 22.1 %collective-permute-start.11 = (bf16[448,1152]{1,0:T(8,128)(2,1)}, bf16[448,1152]{1,0:T(8,128)(2,1)}, u32[]{:S(2)}, u32[]{:S(2)}) collective-permute-start(bf16[448,1152]{1,0:T(8,128)(2,1)} %collective-permute-done.10.refs_0_), channel_id=1, source_target_pairs={{0,16},{8,120},{16,32},{24,8},{32,48},{40,24},{48,64},{56,40},{64,... | collective-permute-start | bytes 3096584 | tf_op jit(solution)/shard_map/ppermute | solution.py:144
  65.3 22.0 %collective-permute-start.5 = (bf16[448,1152]{1,0:T(8,128)(2,1)}, bf16[448,1152]{1,0:T(8,128)(2,1)S(1)}, u32[]{:S(2)}, u32[]{:S(2)}) collective-permute-start(bf16[448,1152]{1,0:T(8,128)(2,1)} %collective-permute-done.4.refs_0_), channel_id=1, source_target_pairs={{0,16},{8,120},{16,32},{24,8},{32,48},{40,24},{48,64},{56,40},{64,... | collective-permute-start | bytes 3096584 | tf_op jit(solution)/shard_map/ppermute | solution.py:144
  66.3 11.0 %collective-permute-start.19 = (bf16[16,56]{1,0:T(8,128)(2,1)S(1)}, bf16[16,56]{1,0:T(8,128)(2,1)S(1)}, u32[]{:S(2)}, u32[]{:S(2)}) collective-permute-start(bf16[16,56]{1,0:T(8,128)(2,1)S(1)} %bitcast.27), channel_id=1, source_target_pairs={{0,1},{1,0},{2,3},{3,2},{4,5},{5,4},{6,7},{7,6},{8,9},{9,8},{10,11... | collective-permute-start | bytes 5384 | tf_op jit(solution)/shard_map/ppermute | solution.py:206
  67.5 28.0 %collective-permute-start.18 = (bf16[448,1152]{1,0:T(8,128)(2,1)S(1)}, bf16[448,1152]{1,0:T(8,128)(2,1)}, u32[]{:S(2)}, u32[]{:S(2)}) collective-permute-start(bf16[448,1152]{1,0:T(8,128)(2,1)S(1)} %pad_maximum_fusion.1.refs_0_), channel_id=1, source_target_pairs={{0,8},{8,0},{16,24},{24,16},{32,40},{40,32},{48,56},{56,48},{64,72... | collective-permute-start | bytes 3096584 | tf_op jit(solution)/shard_map/ppermute | solution.py:135
  68.9 26.7 %collective-permute-start.17 = (bf16[448,1152]{1,0:T(8,128)(2,1)}, bf16[448,1152]{1,0:T(8,128)(2,1)}, u32[]{:S(2)}, u32[]{:S(2)}) collective-permute-start(bf16[448,1152]{1,0:T(8,128)(2,1)} %collective-permute-done.10.refs_0_), channel_id=1, source_target_pairs={{0,8},{8,0},{16,24},{24,16},{32,40},{40,32},{48,56},{56,48},{64,72... | collective-permute-start | bytes 3096584 | tf_op jit(solution)/shard_map/ppermute | solution.py:135
  76.3 22.1 %collective-permute-start.12 = (bf16[448,1152]{1,0:T(8,128)(2,1)}, bf16[448,1152]{1,0:T(8,128)(2,1)}, u32[]{:S(2)}, u32[]{:S(2)}) collective-permute-start(bf16[448,1152]{1,0:T(8,128)(2,1)} %collective-permute-done.11.refs_0_), channel_id=1, source_target_pairs={{0,16},{8,120},{16,32},{24,8},{32,48},{40,24},{48,64},{56,40},{64,... | collective-permute-start | bytes 3096584 | tf_op jit(solution)/shard_map/ppermute | solution.py:144
  77.4 4.0 %collective-permute-start.20 = (bf16[16,112]{1,0:T(8,128)(2,1)S(1)}, bf16[16,112]{1,0:T(8,128)(2,1)S(1)}, u32[]{:S(2)}, u32[]{:S(2)}) collective-permute-start(bf16[16,112]{1,0:T(8,128)(2,1)S(1)} %reshape.39), channel_id=1, source_target_pairs={{0,2},{1,3},{2,0},{3,1},{4,6},{5,7},{6,4},{7,5},{8,10},{9,11},{10,... | collective-permute-start | bytes 10760 | tf_op jit(solution)/shard_map/ppermute | solution.py:206
  88.2 18.9 %collective-permute-start.8 = (bf16[352,1152]{1,0:T(8,128)(2,1)}, bf16[352,1152]{1,0:T(8,128)(2,1)}, u32[]{:S(2)}, u32[]{:S(2)}) collective-permute-start(bf16[352,1152]{1,0:T(8,128)(2,1)} %slice.59), channel_id=1, source_target_pairs={{0,16},{8,120},{16,32},{24,8},{32,48},{40,24},{48,64},{56,40},{64,... | collective-permute-start | bytes 2433032 | tf_op jit(solution)/shard_map/ppermute | solution.py:144
  89.3 4.0 %collective-permute-start.21 = (bf16[16,224]{1,0:T(8,128)(2,1)S(1)}, bf16[16,224]{1,0:T(8,128)(2,1)S(1)}, u32[]{:S(2)}, u32[]{:S(2)}) collective-permute-start(bf16[16,224]{1,0:T(8,128)(2,1)S(1)} %reshape.40), channel_id=1, source_target_pairs={{0,4},{1,5},{2,6},{3,7},{4,0},{5,1},{6,2},{7,3},{8,12},{9,13},{10,... | collective-permute-start | bytes 21512 | tf_op jit(solution)/shard_map/ppermute | solution.py:206
  93.3 17.5 %collective-permute-start.16 = (bf16[448,1152]{1,0:T(8,128)(2,1)}, bf16[448,1152]{1,0:T(8,128)(2,1)}, u32[]{:S(2)}, u32[]{:S(2)}) collective-permute-start(bf16[448,1152]{1,0:T(8,128)(2,1)} %collective-permute-done.4.refs_0_), channel_id=1, source_target_pairs={{0,8},{8,0},{16,24},{24,16},{32,40},{40,32},{48,56},{56,48},{64,72... | collective-permute-start | bytes 3096584 | tf_op jit(solution)/shard_map/ppermute | solution.py:135
  95.6 39.6 %collective-permute-start.15 = (bf16[448,1152]{1,0:T(8,128)(2,1)}, bf16[448,1152]{1,0:T(8,128)(2,1)}, u32[]{:S(2)}, u32[]{:S(2)}) collective-permute-start(bf16[448,1152]{1,0:T(8,128)(2,1)} %collective-permute-done.11.refs_0_), channel_id=1, source_target_pairs={{0,8},{8,0},{16,24},{24,16},{32,40},{40,32},{48,56},{56,48},{64,72... | collective-permute-start | bytes 3096584 | tf_op jit(solution)/shard_map/ppermute | solution.py:135
  95.6 42.8 %collective-permute-start.14 = (bf16[448,1152]{1,0:T(8,128)(2,1)S(1)}, bf16[448,1152]{1,0:T(8,128)(2,1)}, u32[]{:S(2)}, u32[]{:S(2)}) collective-permute-start(bf16[448,1152]{1,0:T(8,128)(2,1)S(1)} %collective-permute-done.5.refs_0_), channel_id=1, source_target_pairs={{0,8},{8,0},{16,24},{24,16},{32,40},{40,32},{48,56},{56,48},{64,72... | collective-permute-start | bytes 3096584 | tf_op jit(solution)/shard_map/ppermute | solution.py:135
  98.4 44.4 %collective-permute-start.13 = (bf16[448,1152]{1,0:T(8,128)(2,1)}, bf16[448,1152]{1,0:T(8,128)(2,1)}, u32[]{:S(2)}, u32[]{:S(2)}) collective-permute-start(bf16[448,1152]{1,0:T(8,128)(2,1)} %collective-permute-done.12.refs_0_), channel_id=1, source_target_pairs={{0,8},{8,0},{16,24},{24,16},{32,40},{40,32},{48,56},{56,48},{64,72... | collective-permute-start | bytes 3096584 | tf_op jit(solution)/shard_map/ppermute | solution.py:135
  107.1 40.0 %collective-permute-start.9 = (bf16[352,1152]{1,0:T(8,128)(2,1)}, bf16[352,1152]{1,0:T(8,128)(2,1)}, u32[]{:S(2)}, u32[]{:S(2)}) collective-permute-start(bf16[352,1152]{1,0:T(8,128)(2,1)} %collective-permute-done.8.refs_0_), channel_id=1, source_target_pairs={{0,8},{8,0},{16,24},{24,16},{32,40},{40,32},{48,56},{56,48},{64,72... | collective-permute-start | bytes 2433032 | tf_op jit(solution)/shard_map/ppermute | solution.py:135
  110.8 5.2 %collective-permute-start.6 = (bf16[96,1152]{1,0:T(8,128)(2,1)S(1)}, bf16[96,1152]{1,0:T(8,128)(2,1)S(1)}, u32[]{:S(2)}, u32[]{:S(2)}) collective-permute-start(bf16[96,1152]{1,0:T(8,128)(2,1)S(1)} %slice.58), channel_id=1, source_target_pairs={{0,16},{8,120},{16,32},{24,8},{32,48},{40,24},{48,64},{56,40},{64,... | collective-permute-start | bytes 663560 | tf_op jit(solution)/shard_map/ppermute | solution.py:144
  116.0 33.2 %collective-permute-start.7 = (bf16[96,1152]{1,0:T(8,128)(2,1)S(1)}, bf16[96,1152]{1,0:T(8,128)(2,1)S(1)}, u32[]{:S(2)}, u32[]{:S(2)}) collective-permute-start(bf16[96,1152]{1,0:T(8,128)(2,1)S(1)} %collective-permute-done.6.refs_0_), channel_id=1, source_target_pairs={{0,8},{8,0},{16,24},{24,16},{32,40},{40,32},{48,56},{56,48},{64,72... | collective-permute-start | bytes 663560 | tf_op jit(solution)/shard_map/ppermute | solution.py:135
  118.8 1.2 copy-start.1
